TPU v7x, 128 devices: a whole 4x4x4 slice. The times are simulated.
128 devices in a mesh: dp: 1, cp: 128 (over z, y, x, core).
Axes of the slice: x: 4, y: 4, z: 4, core: 2. Of those that a mesh axis runs over, the one named last changes fastest.
Arguments:
- x_in: bfloat16 [1, 8192, 16384], P('dp', 'cp')
- seg_ids: int32 [8192], P(('dp', 'cp'))
- positions: int32 [8192], P(('dp', 'cp'))
- attn_gain: bfloat16 [16384], replicated
- w_q: bfloat16 [16384, 2048], replicated
- w_k: bfloat16 [16384, 128], replicated
- w_v: bfloat16 [16384, 128], replicated
- w_o: bfloat16 [2048, 16384], replicated
- mlp_gain: bfloat16 [16384], replicated
- w_gate: bfloat16 [16384, 6656], replicated
- w_up: bfloat16 [16384, 6656], replicated
- w_down: bfloat16 [6656, 16384], replicated
Outputs:
- output 1: bfloat16 [1, 8192, 16384], P('dp', 'cp')
- output 2: bfloat16 [8192, 1, 128], P(('dp', 'cp'))
- output 3: bfloat16 [8192, 1, 128], P(('dp', 'cp'))
All inputs are finite; a program needn't handle non-finite values.
Results may differ from a plain program's by a relative error of at most 0.0125566.
Values are sent between devices in bfloat16 or wider.
A program may use at most 1.5 GiB of HBM per device.

v0:
```python
import jax
import jax.numpy as jnp
from jax import lax
from jax.sharding import PartitionSpec as P

HEAD_DIM = 128
ROPE_THETA = 500000.0
ROPE_FACTOR = 8.0
LOW_FREQ = 1.0
HIGH_FREQ = 4.0
ORIG_CTX = 8192.0
NORM_EPS = 1e-5
NEG_BIG = -1e30


def rope_freqs():
    exponent = jnp.arange(0, HEAD_DIM, 2).astype(jnp.float32) / HEAD_DIM
    inv_freq = 1.0 / (ROPE_THETA ** exponent)
    wavelen = 2.0 * jnp.pi / inv_freq
    smooth = jnp.clip((ORIG_CTX / wavelen - LOW_FREQ) / (HIGH_FREQ - LOW_FREQ), 0.0, 1.0)
    return (1.0 - smooth) * inv_freq / ROPE_FACTOR + smooth * inv_freq


def apply_rope(tensor, cos_t, sin_t):
    half = tensor.shape[-1] // 2
    first = tensor[..., :half]
    second = tensor[..., half:]
    return jnp.concatenate([first * cos_t - second * sin_t, second * cos_t + first * sin_t], axis=-1)


def rms_norm(tensor, gain):
    vec_f32 = tensor.astype(jnp.float32)
    inv_rms = lax.rsqrt(jnp.mean(vec_f32 * vec_f32, axis=-1, keepdims=True) + NORM_EPS)
    return (vec_f32 * inv_rms * gain.astype(jnp.float32)).astype(jnp.bfloat16)


def project_rows(rows, pos_rows, attn_gain, w_q, w_k, w_v):
    count = rows.shape[0]
    kv_heads = w_k.shape[1] // HEAD_DIM
    group_rep = w_q.shape[1] // w_k.shape[1]
    normed = rms_norm(rows, attn_gain)
    angles = pos_rows.astype(jnp.float32)[:, None] * rope_freqs()[None, :]
    cos_t = jnp.cos(angles)[:, None, :]
    sin_t = jnp.sin(angles)[:, None, :]
    q_raw = jnp.dot(normed, w_q, preferred_element_type=jnp.float32).reshape(count, kv_heads * group_rep, HEAD_DIM)
    k_raw = jnp.dot(normed, w_k, preferred_element_type=jnp.float32).reshape(count, kv_heads, HEAD_DIM)
    v_raw = jnp.dot(normed, w_v, preferred_element_type=jnp.float32).reshape(count, kv_heads, HEAD_DIM)
    q_heads = apply_rope(q_raw, cos_t, sin_t).astype(jnp.bfloat16).reshape(count, kv_heads, group_rep, HEAD_DIM)
    k_heads = apply_rope(k_raw, cos_t, sin_t).astype(jnp.bfloat16)
    return q_heads, k_heads, v_raw.astype(jnp.bfloat16)


def attend_block(state, q_heads, seg_rows, pos_rows, k_block, v_block, seg_keys, pos_keys):
    m_run, l_run, acc_run = state
    scores = jnp.einsum('tgrd,ugd->grtu', q_heads, k_block, preferred_element_type=jnp.float32) * (HEAD_DIM ** -0.5)
    visible = (seg_keys[None, :] == seg_rows[:, None]) & (pos_keys[None, :] <= pos_rows[:, None])
    scores = jnp.where(visible, scores, NEG_BIG)
    m_new = jnp.maximum(m_run, jnp.max(scores, axis=-1))
    prob_w = jnp.where(visible, jnp.exp(scores - m_new[..., None]), 0.0)
    rescale = jnp.exp(m_run - m_new)
    l_new = l_run * rescale + jnp.sum(prob_w, axis=-1)
    acc_new = acc_run * rescale[..., None] + jnp.einsum('grtu,ugd->grtd', prob_w.astype(jnp.bfloat16), v_block, preferred_element_type=jnp.float32)
    return m_new, l_new, acc_new


def close_attention(state):
    l_run = state[1]
    kv_heads, group_rep, count = l_run.shape
    out_rows = state[2] / l_run[..., None]
    return out_rows.transpose(2, 0, 1, 3).reshape(count, kv_heads * group_rep * HEAD_DIM).astype(jnp.bfloat16)


def finish_rows(rows, attn_rows, w_o, mlp_gain, w_gate, w_up, w_down):
    resid_mid = (rows.astype(jnp.float32) + jnp.dot(attn_rows, w_o, preferred_element_type=jnp.float32)).astype(jnp.bfloat16)
    normed = rms_norm(resid_mid, mlp_gain)
    gate = jnp.dot(normed, w_gate, preferred_element_type=jnp.float32)
    up_val = jnp.dot(normed, w_up, preferred_element_type=jnp.float32)
    hidden = (jax.nn.silu(gate) * up_val).astype(jnp.bfloat16)
    return (resid_mid.astype(jnp.float32) + jnp.dot(hidden, w_down, preferred_element_type=jnp.float32)).astype(jnp.bfloat16)


def solution(mesh):
    cp_size = mesh.shape['cp']
    shift = [(src, (src + 1) % cp_size) for src in range(cp_size)]

    def device_fn(x_loc, seg_loc, pos_loc, attn_gain, w_q, w_k, w_v, w_o, mlp_gain, w_gate, w_up, w_down):
        rows = x_loc[0]
        q_heads, k_heads, v_heads = project_rows(rows, pos_loc, attn_gain, w_q, w_k, w_v)
        count = q_heads.shape[0]
        kv_heads = q_heads.shape[1]
        group_rep = q_heads.shape[2]
        state = (jnp.full((kv_heads, group_rep, count), NEG_BIG, jnp.float32), jnp.zeros((kv_heads, group_rep, count), jnp.float32), jnp.zeros((kv_heads, group_rep, count, HEAD_DIM), jnp.float32))
        state = attend_block(state, q_heads, seg_loc, pos_loc, k_heads, v_heads, seg_loc, pos_loc)

        def remote_step(step, carry):
            run_state, held = carry
            held = lax.ppermute(held, 'cp', shift)
            run_state = attend_block(run_state, q_heads, seg_loc, pos_loc, held[0], held[1], held[2], held[3])
            return run_state, held

        state = lax.fori_loop(0, cp_size - 1, remote_step, (state, (k_heads, v_heads, seg_loc, pos_loc)))[0]
        attn_rows = close_attention(state)
        z_rows = finish_rows(rows, attn_rows, w_o, mlp_gain, w_gate, w_up, w_down)
        return z_rows[None], k_heads, v_heads

    seq_spec = P(('dp', 'cp'))
    return jax.shard_map(device_fn, mesh=mesh, in_specs=(P('dp', 'cp', None), seq_spec, seq_spec, P(), P(), P(), P(), P(), P(), P(), P(), P()), out_specs=(P('dp', 'cp', None), P(('dp', 'cp'), None, None), P(('dp', 'cp'), None, None)), check_vma=False)
```

profile of v0, /device:TPU:1, one launch (start us, length us, event | category | flops | bytes accessed | tf_op | source)
XLA Modules:
  0.0 1601.5 jit_solution(10106900457577630065)
XLA Ops:
  3.5 81.7 %copy.24 = bf16[2048,16384]{1,0:T(8,128)(2,1)} copy(bf16[2048,16384]{0,1:T(8,128)(2,1)} %bitcast.20) | data formatting | bytes 134217728 | tf_op jit(solution)/shard_map/dot_general | solution.py:45
  85.2 27.1 %fusion.28 = f32[64,16,128]{2,0,1:T(8,128)S(1)} fusion(bf16[16,128,16384]{2,1,0:T(8,128)(2,1)} %bitcast.21, bf16[1,64,16384]{2,1,0:T(8,128)(2,1)S(1)} %copy-done, f32[16384]{0:T(1024)S(1)} %convert_element_type.94, f32[64]{0:T(128)S(1)} %add_rsqrt_fusion.1), kind=kOutput, calls=%fused_computation.41 | convolution fusion | flops 4299161600 | bytes 69796096 | tf_op jit(solution)/shard_map/dot_general | solution.py:45
  119.0 1247.9 %while.22 = (s32[]{:T(128)}, f32[1,16,64]{2,1,0:T(8,128)S(1)}, f32[1,16,64]{2,1,0:T(8,128)S(1)}, f32[1,16,64,128]{3,2,1,0:T(8,128)S(1)}, bf16[64,1,128]{2,0,1:T(...) while((s32[]{:T(128)}, f32[1,16,64]{2,1,0:T(8,128)S(1)}, ...), condition=%wide.region_6.7_spmd, body=%wide.region_3.6_spmd.sunk | while | flops 34421760 | bytes 2412821 | solution.py:101
  153.8 8.3 collective-permute-done.1
  163.6 8.3 collective-permute-done.1
  183.4 8.3 collective-permute-done.1
  203.1 8.3 collective-permute-done.1
  222.8 8.3 collective-permute-done.1
  242.6 8.3 collective-permute-done.1
  262.3 8.3 collective-permute-done.1
  282.0 8.3 collective-permute-done.1
  301.7 8.3 collective-permute-done.1
  321.5 8.3 collective-permute-done.1
  341.2 8.3 collective-permute-done.1
  360.9 8.3 collective-permute-done.1
  380.7 8.3 collective-permute-done.1
  400.4 8.3 collective-permute-done.1
  420.1 8.3 collective-permute-done.1
  439.9 8.3 collective-permute-done.1
  459.6 8.3 collective-permute-done.1
  479.3 8.3 collective-permute-done.1
  499.1 8.3 collective-permute-done.1
  518.8 8.3 collective-permute-done.1
  538.5 8.3 collective-permute-done.1
  558.2 8.3 collective-permute-done.1
  578.0 8.3 collective-permute-done.1
  597.7 8.3 collective-permute-done.1
  617.4 8.3 collective-permute-done.1
  637.2 8.3 collective-permute-done.1
  656.9 8.3 collective-permute-done.1
  676.6 8.3 collective-permute-done.1
  696.4 8.3 collective-permute-done.1
  716.1 8.3 collective-permute-done.1
  735.8 8.3 collective-permute-done.1
  755.6 8.3 collective-permute-done.1
  775.3 8.3 collective-permute-done.1
  795.0 8.3 collective-permute-done.1
  814.7 8.3 collective-permute-done.1
  834.5 8.3 collective-permute-done.1
  952.9 8.3 collective-permute-done.1
  1012.0 8.3 collective-permute-done.1
  1071.2 8.3 collective-permute-done.1
  1130.4 8.3 collective-permute-done.1
  1327.7 8.3 collective-permute-done.1
  1367.3 26.0 %multiply_reduce_fusion = (f32[64]{0:T(128)S(1)}, f32[64,16384]{1,0:T(8,128)}) fusion(bf16[2048,16384]{1,0:T(8,128)(2,1)} %param.21, bf16[8,8,16,128]{3,2,1,0:T(8,128)(2,1)S(1)} %bitcast.132, bf16[1,64,16384]{2,1,0:T(8,128)(2,1)S(1)} %copy-done), kind=kOutput, calls=%fused_computation.39 | convolution fusion | flops 4301258752 | bytes 73662720 | tf_op jit(solution)/shard_map/dot_general | solution.py:74
  1393.3 68.5 %fusion.64 = f32[64,6656]{1,0:T(8,128)S(1)} fusion(bf16[16384,6656]{1,0:T(8,128)(2,1)} %param.23, f32[64,16384]{1,0:T(8,128)} %get-tuple-element.101, f32[16384]{0:T(1024)S(1)} %convert_element_type.109, f32[64]{0:T(128)S(1)} %add_rsqrt_fusion), kind=kOutput, calls=%fused_computation.95 | convolution fusion | flops 13961789440 | bytes 224067840 | tf_op jit(solution)/shard_map/dot_general | solution.py:76
  1461.8 69.7 %fusion.19 = bf16[64,6656]{1,0:T(8,128)(2,1)S(1)} fusion(bf16[16384,6656]{1,0:T(8,128)(2,1)} %param.24, f32[64,6656]{1,0:T(8,128)S(1)} %fusion.64, f32[64,16384]{1,0:T(8,128)} %get-tuple-element.101, f32[16384]{0:T(1024)S(1)} %convert_element_type.109, f32[64]{0:T(128)S(1)} %add_rsqrt_fusion), kind=kOutput, calls=%fused_computation.28 | convolution fusion | flops 13964345344 | bytes 224919808 | tf_op jit(solution)/shard_map/dot_general | solution.py:77
  1531.6 69.9 %fusion.18 = bf16[1,64,16384]{2,1,0:T(8,128)(2,1)} fusion(f32[64,16384]{1,0:T(8,128)} %get-tuple-element.101, bf16[64,6656]{1,0:T(8,128)(2,1)S(1)} %fusion.19, bf16[6656,16384]{1,0:T(8,128)(2,1)} %param.25), kind=kOutput, calls=%fused_computation.26 | convolution fusion | flops 13960740864 | bytes 225247232 | tf_op jit(solution)/shard_map/dot_general | solution.py:79
  (2412 shorter events, 899.2 us)
Async XLA Ops:
  153.7 9.2 collective-permute-start.3
  163.6 9.2 collective-permute-start.3
  183.3 9.2 collective-permute-start.3
  203.0 9.2 collective-permute-start.3
  222.7 9.2 collective-permute-start.3
  242.5 9.2 collective-permute-start.3
  262.2 9.2 collective-permute-start.3
  281.9 9.2 collective-permute-start.3
  301.7 9.2 collective-permute-start.3
  321.4 9.2 collective-permute-start.3
  341.1 9.2 collective-permute-start.3
  360.9 9.2 collective-permute-start.3
  380.6 9.2 collective-permute-start.3
  400.3 9.2 collective-permute-start.3
  420.0 9.2 collective-permute-start.3
  439.8 9.2 collective-permute-start.3
  459.5 9.2 collective-permute-start.3
  479.2 9.2 collective-permute-start.3
  499.0 9.2 collective-permute-start.3
  518.7 9.2 collective-permute-start.3
  538.4 9.2 collective-permute-start.3
  558.2 9.2 collective-permute-start.3
  577.9 9.2 collective-permute-start.3
  597.6 9.2 collective-permute-start.3
  617.4 9.2 collective-permute-start.3
  637.1 9.2 collective-permute-start.3
  656.8 9.2 collective-permute-start.3
  676.5 9.2 collective-permute-start.3
  696.3 9.2 collective-permute-start.3
  716.0 9.2 collective-permute-start.3
  735.7 9.2 collective-permute-start.3
  755.5 9.2 collective-permute-start.3
  775.2 9.2 collective-permute-start.3
  794.9 9.2 collective-permute-start.3
  814.7 9.2 collective-permute-start.3
  834.4 9.2 collective-permute-start.3
  854.1 9.2 collective-permute-start.3
  913.3 9.2 collective-permute-start.3
  972.5 9.2 collective-permute-start.3
  1031.7 9.2 collective-permute-start.3
  1051.4 9.2 collective-permute-start.3
  1090.9 9.2 collective-permute-start.3
  1110.6 9.2 collective-permute-start.3
  1150.1 9.2 collective-permute-start.3
  1169.8 9.2 collective-permute-start.3
  1229.0 9.2 collective-permute-start.3
  1288.2 9.2 collective-permute-start.3
  1347.4 9.2 collective-permute-start.3
  (467 other events, 4116.8 us)
where the time goes:
time: 1610 us; the launch traced here: 1600 us
  waiting for transfers between devices  1050 us (65%)
  matrix products  368 us (23%)
  local copies, waits for them, and re-layouts  84.3 us (5%)
  starting transfers between devices  47.5 us (3%)
  other arithmetic  33 us (2%)
  loops' own time  18.4 us (1%)
    ppermute x508, waiting for transfers between devices, remote_step(): held = lax.ppermute(held, 'cp', shift)  1050 us
    dot_general x1, local copies, waits for them, and re-layouts, project_rows(): jnp.dot(normed, w_q, preferred_element_type=jnp.float32)  81.7 us
    dot_general x1, matrix products, finish_rows(): jnp.dot(hidden, w_down, preferred_element_type=jnp.float32)  69.9 us
    dot_general x1, matrix products, finish_rows(): up_val = jnp.dot(normed, w_up, preferred_element_type=jnp.float32)  69.7 us
    dot_general x1, matrix products, finish_rows(): gate = jnp.dot(normed, w_gate, preferred_element_type=jnp.float32)  68.5 us
    dot_general x128, matrix products, attend_block(): jnp.einsum('grtu,ugd->grtd', prob_w.astype(jnp.bfloat16), v_block, prefer...  52.8 us
    dot_general x128, matrix products, attend_block(): jnp.einsum('tgrd,ugd->grtu', q_heads, k_block, preferred_element_type=jnp...  49.7 us
    ppermute x508, starting transfers between devices, remote_step(): held = lax.ppermute(held, 'cp', shift)  47.5 us
  transfers between devices with their start and end apart: 508, of which 253 were waited for; matrix products, arithmetic and copies ran while one was open for 5% of the time, Pallas kernels for 0%

commit v1 on v0

v1 whole, which is shorter than its diff:
```python
import functools
import math

import jax
import jax.numpy as jnp
from jax import lax
from jax.experimental import pallas as pl
from jax.experimental.pallas import tpu as pltpu
from jax.sharding import PartitionSpec as P

MODEL = 16384
HALF = MODEL // 2
HEADS = 16
HEAD_DIM = 128
QCOLS = HEADS * HEAD_DIM // 2
FF = 6656
FFH = FF // 2
ROWS = 64
CHUNK = 32
PAIR = 2 * ROWS
SEQ = 8192
ROPE_THETA = 500000.0
ROPE_FACTOR = 8.0
LOW_FREQ = 1.0
HIGH_FREQ = 4.0
ORIG_CTX = 8192.0
NORM_EPS = 1e-5
NEG_BIG = -1e30
EXP_SCALE = HEAD_DIM ** -0.5 * math.log2(math.e)

N1 = 5
N2 = 10
KC = 512
NB = 2048
Q_TRIPS = MODEL // (2 * KC)
O_TRIPS = (HALF // NB) * (HEADS * HEAD_DIM // KC)
D_K = FF // KC
D_TRIPS = (HALF // NB) * D_K
G_TRIPS = MODEL // KC
KV_PER_SLOT = FFH // 256
KV_PIECES = MODEL // KC
HOOK_B, HOOK_C = 5, 13

MESH = pl.DeviceIdType.MESH
F32 = jnp.float32
BF16 = jnp.bfloat16
BLOCKS = ((0, 0, 'yzx'), (1, 0, 'zxy'), (0, 1, 'xyz'), (1, 1, 'xyz'))


def rope_tables(pos, lanes=HEAD_DIM):
    lane = lax.broadcasted_iota(jnp.int32, (8, lanes), 1)
    j = lax.rem(lane, HEAD_DIM // 2).astype(F32)
    inv_freq = jnp.exp(j * (-2.0 / HEAD_DIM * math.log(ROPE_THETA)))
    wavelen = (2.0 * math.pi) / inv_freq
    smooth = jnp.clip((ORIG_CTX / wavelen - LOW_FREQ) / (HIGH_FREQ - LOW_FREQ), 0.0, 1.0)
    freq = ((1.0 - smooth) * inv_freq / ROPE_FACTOR + smooth * inv_freq)[0:1]
    angle = pos * freq
    sign = jnp.where(lane[0:1] < HEAD_DIM // 2, -1.0, 1.0)
    return jnp.cos(angle), jnp.sin(angle) * sign


def rope(t, cos_t, sin_t):
    return t * cos_t + pltpu.roll(t, HEAD_DIM // 2, 1) * sin_t


def layer_kernel(x_hbm, pos_ref, ag_ref, wq, wk, wv, wo, mg_ref, wg, wu, wd,
                 z_hbm, k_out, v_out,
                 x128, bbuf, kv, w1, w2, acc, acc_g, acc_u, qs, att, ml, obuf, mbuf, st, ss, zst, kst,
                 xl_sem, xs_sem, xr_sem, sts_sem, str_sem, kvw_sem, w1_sem, w2_sem, gs_sem, gr_sem, fs_sem, fr_sem,
                 os_sem, or_sem, sss_sem, ssr_sem, bs_sem, br_sem, ms_sem, mr_sem, zl_sem, zs_sem, zr_sem, ko_sem):
    me = lax.axis_index('cp')
    core = lax.rem(me, 2)
    chip = lax.div(me, 2)
    coords = {'x': lax.rem(chip, 4), 'y': lax.rem(lax.div(chip, 4), 4), 'z': lax.div(chip, 16)}
    sib = me + 1 - 2 * core
    other = 1 - core

    def peer(dim, k):
        c = dict(coords)
        c[dim] = lax.rem(c[dim] + k, 4)
        return ((c['z'] * 4 + c['y']) * 4 + c['x']) * 2 + core

    def remote(src, dst, s, r, dev):
        return pltpu.make_async_remote_copy(src, dst, s, r, device_id={'cp': dev}, device_id_type=MESH)

    def to_sib(src, dst, s, r):
        return remote(src, dst, s, r, sib)

    own_rows = pl.ds(pl.multiple_of(core * ROWS, ROWS), ROWS)
    sib_rows = pl.ds(pl.multiple_of(other * ROWS, ROWS), ROWS)
    own_half = pl.multiple_of(core * HALF, HALF)
    sib_half = pl.multiple_of(other * HALF, HALF)

    def kv_dst(c, width):
        return w1.at[lax.div(c, KV_PER_SLOT), :, pl.ds(pl.multiple_of(lax.rem(c, KV_PER_SLOT) * 256 + (128 if width == -128 else 0), 128), abs(width))]

    def kv_start(c):
        rows = pl.ds(pl.multiple_of(c * KC, KC), KC)
        pltpu.make_async_copy(wk.at[rows, :], kv_dst(c, 128), kvw_sem.at[c]).start()
        pltpu.make_async_copy(wv.at[rows, :], kv_dst(c, -128), kvw_sem.at[c]).start()

    def kv_wait(c):
        pltpu.make_async_copy(wq.at[pl.ds(0, KC), pl.ds(0, 256)], kv_dst(c, 256), kvw_sem.at[c]).wait()

    def w2_start(n):
        slot = lax.rem(n, N2)

        @pl.when(n < Q_TRIPS)
        def _():
            for h in range(2):
                rows = pl.ds(pl.multiple_of(n * (2 * KC) + h * KC, KC), KC)
                cols = pl.ds(pl.multiple_of(core * QCOLS, QCOLS), QCOLS)
                pltpu.make_async_copy(wq.at[rows, cols], w2.at[slot, :, pl.ds(h * QCOLS, QCOLS)], w2_sem.at[slot]).start()

        @pl.when((n >= Q_TRIPS) & (n < Q_TRIPS + O_TRIPS))
        def _():
            rows = pl.ds(pl.multiple_of(o_chunk(n - Q_TRIPS) * KC, KC), KC)
            cols = pl.ds(pl.multiple_of(own_half + lax.div(n - Q_TRIPS, 4) * NB, NB), NB)
            pltpu.make_async_copy(wo.at[rows, cols], w2.at[slot], w2_sem.at[slot]).start()

        @pl.when((n >= Q_TRIPS + O_TRIPS) & (n < Q_TRIPS + O_TRIPS + D_TRIPS))
        def _():
            i = n - (Q_TRIPS + O_TRIPS)
            rows = pl.ds(pl.multiple_of(d_chunk(lax.rem(i, D_K)) * KC, KC), KC)
            cols = pl.ds(pl.multiple_of(own_half + lax.div(i, D_K) * NB, NB), NB)
            pltpu.make_async_copy(wd.at[rows, cols], w2.at[slot], w2_sem.at[slot]).start()

    def w2_wait(n):
        slot = lax.rem(n, N2)
        pltpu.make_async_copy(wo.at[pl.ds(0, KC), pl.ds(0, NB)], w2.at[slot], w2_sem.at[slot]).wait()
        return slot

    def o_chunk(i):
        kk = lax.rem(i, 4)
        return lax.rem(kk + 2 * core, 4)

    def d_chunk(kk):
        late = jnp.where(kk < 6, kk + 7, jnp.where(kk == 6, 6, kk - 7))
        return jnp.where(core == 0, kk, late)

    def g_chunk(i):
        return lax.rem(i + core * (G_TRIPS // 2), G_TRIPS)

    def w1_start(n):
        slot = lax.rem(n, N1)
        rows = pl.ds(pl.multiple_of(g_chunk(lax.div(n, 2)) * KC, KC), KC)
        cols = pl.ds(pl.multiple_of(core * FFH, FFH), FFH)

        @pl.when((n < 2 * G_TRIPS) & (lax.rem(n, 2) == 0))
        def _():
            pltpu.make_async_copy(wg.at[rows, cols], w1.at[slot], w1_sem.at[slot]).start()

        @pl.when((n < 2 * G_TRIPS) & (lax.rem(n, 2) == 1))
        def _():
            pltpu.make_async_copy(wu.at[rows, cols], w1.at[slot], w1_sem.at[slot]).start()

    def w1_wait(n):
        slot = lax.rem(n, N1)
        pltpu.make_async_copy(wg.at[pl.ds(0, KC), pl.ds(0, FFH)], w1.at[slot], w1_sem.at[slot]).wait()
        return slot

    x_local = pltpu.make_async_copy(x_hbm, x128.at[own_rows, :], xl_sem)
    x_local.start()

    @pl.loop(0, KV_PIECES)
    def _(c):
        kv_start(c)

    @pl.loop(0, N2)
    def _(n):
        w2_start(n)

    barrier = pltpu.get_barrier_semaphore()
    pl.semaphore_signal(barrier, inc=1, device_id={'cp': sib}, device_id_type=MESH)
    for dim in 'xyz':
        for k in (1, 2, 3):
            pl.semaphore_signal(barrier, inc=1, device_id={'cp': peer(dim, k)}, device_id_type=MESH)
    pl.semaphore_wait(barrier, 10)

    XP = 4

    def x_copy(i):
        cols = pl.ds(i * (MODEL // XP), MODEL // XP)
        return to_sib(x_hbm.at[:, cols], x128.at[own_rows, cols], xs_sem.at[i], xr_sem.at[i])

    for i in range(XP):
        x_copy(i).start()

    x_local.wait()

    def square_sum(i, part):
        for u in range(8):
            v = x128[own_rows, pl.ds(pl.multiple_of(i * 1024 + u * 128, 128), 128)].astype(F32)
            part = part + v * v
        return part

    part = lax.fori_loop(0, MODEL // 1024, square_sum, jnp.zeros((ROWS, 128), F32))
    inv_own = lax.rsqrt(jnp.sum(part, axis=1, keepdims=True) / MODEL + NORM_EPS)
    eye = lax.broadcasted_iota(jnp.int32, (ROWS, ROWS), 0) == lax.broadcasted_iota(jnp.int32, (ROWS, ROWS), 1)
    pos_own = jnp.sum(jnp.where(eye, jnp.broadcast_to(pos_ref[...].astype(F32), (ROWS, ROWS)), 0.0), axis=1, keepdims=True)
    lane = lax.broadcasted_iota(jnp.int32, (ROWS, 128), 1)
    st[core] = jnp.where(lane == 0, inv_own, pos_own)
    st_copy = to_sib(st.at[core], st.at[core], sts_sem, str_sem)
    st_copy.start()

    def normalize(rows, inv, lo, hi):
        @pl.loop(lo, hi)
        def _(i):
            for u in range(4):
                cols = pl.ds(pl.multiple_of(i * 1024 + u * 256, 256), 256)
                v = x128[rows, cols].astype(F32) * inv * ag_ref[:, cols].astype(F32)
                bbuf[rows, cols] = v.astype(BF16)

    normalize(own_rows, inv_own, 0, MODEL // 1024)

    def kv_trip(i, total):
        for u in range(8):
            kv_wait(i * 8 + u)
        for u in range(8):
            c = i * 8 + u
            w = w1[lax.div(c, KV_PER_SLOT), :, pl.ds(pl.multiple_of(lax.rem(c, KV_PER_SLOT) * 256, 256), 256)]
            a = bbuf[own_rows, pl.ds(pl.multiple_of(c * KC, KC), KC)]
            total = total + jnp.dot(a, w, preferred_element_type=F32)
        return total

    kv_raw = lax.fori_loop(0, KV_PIECES // 8, kv_trip, jnp.zeros((ROWS, 256), F32))
    cos_own, sin_own = rope_tables(pos_own)
    k_own = rope(kv_raw[:, :128], cos_own, sin_own).astype(BF16)
    v_own = kv_raw[:, 128:].astype(BF16)
    kst[0] = k_own
    kst[1] = v_own
    r0 = (pl.multiple_of(core * CHUNK, CHUNK), pl.multiple_of(other * CHUNK, CHUNK))
    cx, cy, cz = coords['x'], coords['y'], coords['z']
    for i, t in enumerate((k_own, v_own)):
        kv[i, 0, cz, cy, cx, pl.ds(r0[0], CHUNK), :] = t[:CHUNK]
        kv[i, 1, cz, cy, cx, pl.ds(r0[1], CHUNK), :] = t[CHUNK:]
    k_store = pltpu.make_async_copy(kst.at[0], k_out, ko_sem.at[0])
    v_store = pltpu.make_async_copy(kst.at[1], v_out, ko_sem.at[1])
    k_store.start()
    v_store.start()

    def piece(b, pos, full):
        i, half, _ = BLOCKS[b]
        idx = [slice(None) if d in full else pos[d] for d in 'zyx']
        return kv.at[(i, half, *idx, pl.ds(r0[half], CHUNK), slice(None))]

    def from_peer(b, ph, k):
        dims = BLOCKS[b][2]
        pos = dict(coords)
        pos[dims[ph]] = lax.rem(pos[dims[ph]] + 4 - k, 4)
        return piece(b, pos, dims[:ph])

    def guarded(b, ph, k, side, action):
        if ph == 2 and BLOCKS[b][1] == 1:
            pl.when(cz + k >= 4 if side == 'send' else cz < k)(action)
        else:
            action()

    def gather_copy(b, ph, k):
        dims = BLOCKS[b][2]
        src = piece(b, coords, dims[:ph])
        return remote(src, src, gs_sem.at[b, ph, k - 1], gr_sem.at[b, ph, k - 1], peer(dims[ph], k))

    def own_forward(b):
        src = piece(b, coords, '')
        return to_sib(src, src, fs_sem.at[b, 9], fr_sem.at[b, 9])

    def sib_own(b):
        i, half, _ = BLOCKS[b]
        dst = kv.at[i, half, cz, cy, cx, pl.ds(r0[1 - half], CHUNK), :]
        return to_sib(dst, dst, fs_sem.at[b, 9], fr_sem.at[b, 9])

    def forward(b, ph, k):
        src = from_peer(b, ph, k)
        return to_sib(src, src, fs_sem.at[b, ph * 3 + k - 1], fr_sem.at[b, ph * 3 + k - 1])

    def phase_start(ph):
        for b in range(4):
            for k in (1, 2, 3):
                guarded(b, ph, k, 'send', lambda b=b, k=k: gather_copy(b, ph, k).start())

    def phase_finish(ph):
        for b in range(4):
            for k in (1, 2, 3):
                def got(b=b, k=k):
                    gather_copy(b, ph, k).wait_recv()
                    forward(b, ph, k).start()
                guarded(b, ph, k, 'recv', got)
        for b in range(4):
            for k in (1, 2, 3):
                guarded(b, ph, k, 'send', lambda b=b, k=k: gather_copy(b, ph, k).wait_send())

    phase_start(0)
    for b in range(4):
        own_forward(b).start()

    st_copy.wait()
    inv_sib = st[other][:, 0:1]
    for i in range(XP):
        x_copy(i).wait()
        normalize(sib_rows, inv_sib, i * 4, i * 4 + 4)

    acc[...] = jnp.zeros_like(acc)

    @pl.loop(0, Q_TRIPS)
    def _(i):
        @pl.when(i == HOOK_B)
        def _():
            phase_finish(0)
            phase_start(1)

        @pl.when(i == HOOK_C)
        def _():
            phase_finish(1)
            phase_start(2)

        slot = w2_wait(i)
        k0 = pl.multiple_of(i * (2 * KC), 2 * KC)
        acc[:, :QCOLS] += (jnp.dot(bbuf[:, pl.ds(k0, KC)], w2[slot, :, :QCOLS], preferred_element_type=F32)
                           + jnp.dot(bbuf[:, pl.ds(k0 + KC, KC)], w2[slot, :, QCOLS:], preferred_element_type=F32))
        w2_start(i + N2)

    @pl.loop(0, N1)
    def _(n):
        w1_start(n)

    pos_all = jnp.concatenate([st[0][:, 1:2], st[1][:, 1:2]], axis=0)
    cos_t, sin_t = rope_tables(pos_all)
    for h in range(HEADS // 2):
        q = rope(acc[:, h * 128:(h + 1) * 128], cos_t, sin_t).astype(BF16)
        qs[0, h, :CHUNK] = q[:32]
        qs[0, h, CHUNK:] = q[64:96]
        qs[1, h, :CHUNK] = q[96:]
        qs[1, h, CHUNK:] = q[32:64]

    phase_finish(2)
    for b in range(4):
        own_forward(b).wait_send()
        sib_own(b).wait_recv()
    for ph in range(3):
        for b in range(4):
            for k in (1, 2, 3):
                def passed(b=b, ph=ph, k=k):
                    forward(b, ph, k).wait_send()
                    sib_piece(b, ph, k).wait_recv()

                def sib_piece(b, ph, k):
                    i, half, dims = BLOCKS[b]
                    pos = dict(coords)
                    pos[dims[ph]] = lax.rem(pos[dims[ph]] + 4 - k, 4)
                    idx = [slice(None) if d in dims[:ph] else pos[d] for d in 'zyx']
                    dst = kv.at[(i, half, *idx, pl.ds(r0[1 - half], CHUNK), slice(None))]
                    return to_sib(dst, dst, fs_sem.at[b, ph * 3 + k - 1], fr_sem.at[b, ph * 3 + k - 1])
                guarded(b, ph, k, 'recv', passed)

    ml[:, 0] = jnp.full((2, 512, 128), NEG_BIG, F32)
    ml[:, 1] = jnp.zeros((2, 512, 128), F32)
    att[...] = jnp.zeros_like(att)
    c8 = lax.div(chip, 8)

    @pl.loop(0, 17)
    def _(s):
        late_q = s > c8
        late_k = late_q & (s < 9)
        t = jnp.where(late_q, jnp.where(late_k, s - 1, s - 9), c8 - s)
        qh = late_q.astype(jnp.int32)
        kh = late_k.astype(jnp.int32)
        tz, ty = lax.div(t, 2), lax.rem(t, 2) * 2
        keys = kv[0, kh, tz, pl.ds(ty, 2)].reshape(512, 128)
        vals = kv[1, kh, tz, pl.ds(ty, 2)].reshape(512, 128)
        q = qs[qh].reshape(512, 128)
        scores = lax.dot_general(q, keys, (((1,), (1,)), ((), ())), preferred_element_type=F32)
        u = lax.broadcasted_iota(jnp.int32, (1, 512), 1)
        back = lax.div(u, 64)
        key_nat = jnp.where(late_k, SEQ - 64 * (8 * t + 1) - 128 * back + u, 512 * t + u)
        row = lax.broadcasted_iota(jnp.int32, (64, 1), 0)
        row_nat = jnp.where(late_q, SEQ - 64 * (chip + 1), 64 * chip) + row
        pos_e = jnp.concatenate([st[0][:32, 1:2], st[1][:32, 1:2]], axis=0)
        pos_l = jnp.concatenate([st[1][32:, 1:2], st[0][32:, 1:2]], axis=0)
        row_first = row_nat - jnp.where(late_q, pos_l, pos_e).astype(jnp.int32)
        visible = (key_nat >= row_first) & (key_nat <= row_nat)
        scores = jnp.where(visible[None], scores.reshape(8, 64, 512), NEG_BIG).reshape(512, 512)
        m_old = ml[qh, 0]
        m_new = jnp.maximum(m_old, jnp.max(scores, axis=1, keepdims=True))
        p = jnp.exp2((scores - m_new[:, :1]) * EXP_SCALE)
        alpha = jnp.exp2((m_old - m_new) * EXP_SCALE)
        ml[qh, 0] = m_new
        ml[qh, 1] = ml[qh, 1] * alpha + jnp.sum(p, axis=1, keepdims=True)
        att[qh] = att[qh] * alpha + jnp.dot(p.astype(BF16), vals, preferred_element_type=F32)

    for h in range(HEADS // 2):
        r = slice(h * 64, (h + 1) * 64)
        cols = slice(h * 128, (h + 1) * 128)
        o_e = (att[0, r] / ml[0, 1, r]).astype(BF16)
        o_l = (att[1, r] / ml[1, 1, r]).astype(BF16)
        obuf[core, 0:32, cols] = o_e[:32]
        obuf[core, 64:96, cols] = o_e[32:]
        obuf[core, 96:128, cols] = o_l[:32]
        obuf[core, 32:64, cols] = o_l[32:]
    o_copy = to_sib(obuf.at[core], obuf.at[core], os_sem, or_sem)
    o_copy.start()

    ss[core] = jnp.zeros((PAIR, 128), F32)
    acc[...] = jnp.zeros_like(acc)

    @pl.loop(0, O_TRIPS)
    def _(i):
        @pl.when(i == 2)
        def _():
            o_copy.wait()

        slot = w2_wait(Q_TRIPS + i)
        ch = o_chunk(i)
        a = obuf[lax.div(ch, 2), :, pl.ds(pl.multiple_of(lax.rem(ch, 2) * KC, KC), KC)]
        acc[...] += jnp.dot(a, w2[slot], preferred_element_type=F32)
        w2_start(Q_TRIPS + i + N2)

        @pl.when(lax.rem(i, 4) == 3)
        def _():
            n = lax.div(i, 4)

            def column(j, part):
                cols = pl.ds(pl.multiple_of(own_half + n * NB + j * 128, 128), 128)
                local = pl.ds(pl.multiple_of(j * 128, 128), 128)
                h = (x128[:, cols].astype(F32) + acc[:, local]).astype(BF16)
                x128[:, cols] = h
                acc[:, local] = jnp.zeros((PAIR, 128), F32)
                hf = h.astype(F32)
                return part + hf * hf

            ss[core] += lax.fori_loop(0, NB // 128, column, jnp.zeros((PAIR, 128), F32))

    ss_copy = to_sib(ss.at[core], ss.at[core], sss_sem, ssr_sem)
    ss_copy.start()
    ss_copy.wait()
    inv_h = lax.rsqrt(jnp.sum(ss[0] + ss[1], axis=1, keepdims=True) / MODEL + NORM_EPS)

    BP = HALF // NB

    def b_copy(i):
        cols = pl.ds(pl.multiple_of(own_half + i * NB, NB), NB)
        return to_sib(bbuf.at[:, cols], bbuf.at[:, cols], bs_sem.at[i], br_sem.at[i])

    def b_arrival(i):
        cols = pl.ds(pl.multiple_of(sib_half + i * NB, NB), NB)
        return to_sib(bbuf.at[:, cols], bbuf.at[:, cols], bs_sem.at[i], br_sem.at[i])

    for i in range(BP):
        @pl.loop(0, NB // 256)
        def _(j):
            cols = pl.ds(pl.multiple_of(own_half + i * NB + j * 256, 256), 256)
            bbuf[:, cols] = (x128[:, cols].astype(F32) * inv_h * mg_ref[:, cols].astype(F32)).astype(BF16)
        b_copy(i).start()

    acc_g[...] = jnp.zeros_like(acc_g)
    acc_u[...] = jnp.zeros_like(acc_u)

    @pl.loop(0, G_TRIPS)
    def _(i):
        for q in range(BP):
            @pl.when(i == G_TRIPS // 2 + q * (NB // KC))
            def _():
                b_arrival(q).wait_recv()

        a = bbuf[:, pl.ds(pl.multiple_of(g_chunk(i) * KC, KC), KC)]
        sg = w1_wait(2 * i)
        acc_g[...] += jnp.dot(a, w1[sg], preferred_element_type=F32)
        w1_start(2 * i + N1)
        su = w1_wait(2 * i + 1)
        acc_u[...] += jnp.dot(a, w1[su], preferred_element_type=F32)
        w1_start(2 * i + 1 + N1)

    @pl.loop(0, FFH // 256)
    def _(j):
        local = pl.ds(pl.multiple_of(j * 256, 256), 256)
        g = acc_g[:, local]
        m = g * (1.0 / (1.0 + jnp.exp(-g))) * acc_u[:, local]
        mbuf[:, pl.ds(pl.multiple_of(core * FFH + j * 256, 256), 256)] = m.astype(BF16)

    m_cols = pl.ds(pl.multiple_of(core * FFH, FFH), FFH)
    m_copy = to_sib(mbuf.at[:, m_cols], mbuf.at[:, m_cols], ms_sem, mr_sem)
    m_copy.start()

    acc[...] = jnp.zeros_like(acc)

    def z_cols(n):
        return pl.ds(pl.multiple_of(own_half + n * NB, NB), NB)

    def z_local(n):
        return pltpu.make_async_copy(zst.at[lax.rem(n, 2), own_rows, :], z_hbm.at[:, z_cols(n)], zl_sem.at[lax.rem(n, 2)])

    def z_remote(n):
        return to_sib(zst.at[lax.rem(n, 2), sib_rows, :], z_hbm.at[:, z_cols(n)], zs_sem.at[lax.rem(n, 2)], zr_sem.at[n])

    def z_arrival(n):
        cols = pl.ds(pl.multiple_of(sib_half + n * NB, NB), NB)
        return to_sib(zst.at[lax.rem(n, 2), sib_rows, :], z_hbm.at[:, cols], zs_sem.at[lax.rem(n, 2)], zr_sem.at[n])

    @pl.loop(0, D_TRIPS)
    def _(i):
        @pl.when(i == 6)
        def _():
            m_copy.wait()

        n, kk = lax.div(i, D_K), lax.rem(i, D_K)
        slot = w2_wait(Q_TRIPS + O_TRIPS + i)
        a = mbuf[:, pl.ds(pl.multiple_of(d_chunk(kk) * KC, KC), KC)]
        acc[...] += jnp.dot(a, w2[slot], preferred_element_type=F32)
        w2_start(Q_TRIPS + O_TRIPS + i + N2)

        @pl.when(kk == D_K - 1)
        def _():
            @pl.when(n >= 2)
            def _():
                z_local(n - 2).wait()
                z_remote(n - 2).wait_send()

            zslot = lax.rem(n, 2)

            @pl.loop(0, NB // 256)
            def _(j):
                cols = pl.ds(pl.multiple_of(own_half + n * NB + j * 256, 256), 256)
                local = pl.ds(pl.multiple_of(j * 256, 256), 256)
                zst[zslot, :, local] = (x128[:, cols].astype(F32) + acc[:, local]).astype(BF16)
                acc[:, local] = jnp.zeros((PAIR, 256), F32)

            z_local(n).start()
            z_remote(n).start()

    for n in range(HALF // NB):
        if n >= HALF // NB - 2:
            z_local(n).wait()
            z_remote(n).wait_send()
        z_arrival(n).wait_recv()
        b_copy(n).wait_send()
    k_store.wait()
    v_store.wait()


def solution(mesh):
    def device_fn(x_loc, seg_loc, pos_loc, attn_gain, w_q, w_k, w_v, w_o, mlp_gain, w_gate, w_up, w_down):
        any_space = pl.BlockSpec(memory_space=pl.ANY)
        vmem = pl.BlockSpec(memory_space=pltpu.VMEM)
        dma = pltpu.SemaphoreType.DMA
        z_rows, k_rows, v_rows = pl.pallas_call(
            layer_kernel,
            out_shape=(jax.ShapeDtypeStruct((ROWS, MODEL), BF16), jax.ShapeDtypeStruct((ROWS, HEAD_DIM), BF16), jax.ShapeDtypeStruct((ROWS, HEAD_DIM), BF16)),
            in_specs=[any_space, vmem, vmem, any_space, any_space, any_space, any_space, vmem, any_space, any_space, any_space],
            out_specs=(any_space, any_space, any_space),
            scratch_shapes=[
                pltpu.VMEM((PAIR, MODEL), BF16),
                pltpu.VMEM((PAIR, MODEL), BF16),
                pltpu.VMEM((2, 2, 4, 4, 4, 64, 128), BF16),
                pltpu.VMEM((N1, KC, FFH), BF16),
                pltpu.VMEM((N2, KC, NB), BF16),
                pltpu.VMEM((PAIR, NB), F32),
                pltpu.VMEM((PAIR, FFH), F32),
                pltpu.VMEM((PAIR, FFH), F32),
                pltpu.VMEM((2, HEADS // 2, 64, 128), BF16),
                pltpu.VMEM((2, 512, 128), F32),
                pltpu.VMEM((2, 2, 512, 128), F32),
                pltpu.VMEM((2, PAIR, QCOLS), BF16),
                pltpu.VMEM((PAIR, FF), BF16),
                pltpu.VMEM((2, ROWS, 128), F32),
                pltpu.VMEM((2, PAIR, 128), F32),
                pltpu.VMEM((2, PAIR, NB), BF16),
                pltpu.VMEM((2, ROWS, 128), BF16),
                dma, dma((4,)), dma((4,)), dma, dma, dma((KV_PIECES,)), dma((N1,)), dma((N2,)),
                dma((4, 3, 3)), dma((4, 3, 3)), dma((4, 10)), dma((4, 10)),
                dma, dma, dma, dma, dma((4,)), dma((4,)), dma, dma, dma((2,)), dma((2,)), dma((4,)), dma((2,)),
            ],
            compiler_params=pltpu.CompilerParams(collective_id=0, has_side_effects=True, vmem_limit_bytes=67043328),
            name='layer',
        )(x_loc[0], pos_loc.reshape(1, ROWS), attn_gain.reshape(1, MODEL), w_q, w_k, w_v, w_o, mlp_gain.reshape(1, MODEL), w_gate, w_up, w_down)
        return z_rows[None], k_rows[:, None, :], v_rows[:, None, :]

    seq_spec = P(('dp', 'cp'))
    return jax.shard_map(device_fn, mesh=mesh, in_specs=(P('dp', 'cp', None), seq_spec, seq_spec, P(), P(), P(), P(), P(), P(), P(), P(), P()), out_specs=(P('dp', 'cp', None), P(('dp', 'cp'), None, None), P(('dp', 'cp'), None, None)), check_vma=False)
```

time: 1610 us -> 167 us (0.10)
  waiting for transfers between devices: 1050 us -> 0 us
  matrix products: 368 us -> 0 us
  Pallas kernels: 0 us -> 157 us
  local copies, waits for them, and re-layouts: 84.3 us -> 8.54 us
  starting transfers between devices: 47.5 us -> 0 us
  other arithmetic: 33 us -> 0 us
  loops' own time: 18.4 us -> 0 us
    ppermute x508 -> x0, waiting for transfers between devices: 1050 us -> none  [remote_step(): held = lax.ppermute(held, 'cp', shift)]
    dot_general x263 -> x0, matrix products: 368 us -> none  [the longest x1 69.9 us: finish_rows(): jnp.dot(hidden, w_down, preferred_element_type=jnp.float32)]
    pallas_call x0 -> x1, Pallas kernels: none -> 157 us  [device_fn(): pl.pallas_call(layer_kernel, out_shape=(jax.ShapeDtypeStruct((ROWS, MODEL...]
    dot_general x1 -> x0, local copies, waits for them, and re-layouts: 81.7 us -> none  [project_rows(): jnp.dot(normed, w_q, preferred_element_type=jnp.float32)]
    ppermute x508 -> x0, starting transfers between devices: 47.5 us -> none  [remote_step(): held = lax.ppermute(held, 'cp', shift)]
    another operation x1 -> x0, loops' own time: 18.4 us -> none  [device_fn(): lax.fori_loop(0, cp_size - 1, remote_step, (state, (k_heads, v_heads, seg...]
    reduce_sum x129 -> x0, other arithmetic: 18.1 us -> none  [the longest x128 16 us: attend_block(): l_new = l_run * rescale + jnp.sum(prob_w, axis=-1)]
  transfers between devices with their start and end apart: 508 -> 0, of which waited for: 253 -> 0; matrix products, arithmetic and copies ran while one was open for 5% -> 0% of each run, Pallas kernels for 0% -> 0%
where the time goes in v1:
time: 167 us
  Pallas kernels  157 us (94%)
  local copies, waits for them, and re-layouts  8.54 us (5%)
    pallas_call x1, Pallas kernels, device_fn(): pl.pallas_call(layer_kernel, out_shape=(jax.ShapeDtypeStruct((ROWS, MODEL...  157 us
    unnamed x3, local copies, waits for them, and re-layouts  5.69 us

profile of v1, /device:TPU:1, one launch (start us, length us, event | category | flops | bytes accessed | tf_op | source)
XLA Modules:
  0.0 166.5 jit_solution(5471357798254960355)
XLA Ops:
  0.6 1.4 reshape.16.ag_ref
  2.1 1.4 reshape.17.mg_ref
  3.5 157.3 %layer.1 = (bf16[64,16384]{1,0:T(8,128)(2,1)}, bf16[64,128]{1,0:T(8,128)(2,1)}, bf16[64,128]{1,0:T(8,128)(2,1)}) custom-call(bf16[64,16384]{1,0:T(8,128)(2,1)} %bitcast.5, s32[1,64]{1,0:T(1,128)} %bitcast.9, bf16[1,16384]{1,0:T(2,128)(2,1)} %reshape.16.ag_ref, bf16[16384,2048]{1,0:T(8,128)(2,1)} %wq.1, bf16[16384,128]{1,0:T(8,128)(2,1)} %wk.1, ...), custom_call_target="tpu_custom_call" | custom-call | tf_op jit(solution)/shard_map/layer/pallas_call | solution.py:545
  160.8 3.0 %copy.17 = bf16[1,64,16384]{2,1,0:T(8,128)(2,1)} copy(bf16[1,64,16384]{2,1,0:T(8,128)(2,1)} %bitcast.6) | data formatting | bytes 4194304
  163.9 1.3 copy.18
  165.2 1.3 copy.19

commit v2 on v0

v2 whole, which is shorter than its diff:
```python
import functools
import math

import jax
import jax.numpy as jnp
from jax import lax
from jax.experimental import pallas as pl
from jax.experimental.pallas import tpu as pltpu
from jax.sharding import PartitionSpec as P

LANES = 128
SUBLANES = 8
SIDE = 4
MODEL = 16384
HALF = MODEL // 2
HEADS = 16
PAIR_HEADS = HEADS // 4
HEAD_DIM = LANES
QCOLS = HEADS * HEAD_DIM // 2
FF = 6656
FFH = FF // 2
FFQ = FF // 4
ROWS = 64
CHUNK = 32
PAIR = 2 * ROWS
SEQ = 8192
ROPE_THETA = 500000.0
ROPE_FACTOR = 8.0
LOW_FREQ = 1.0
HIGH_FREQ = 4.0
ORIG_CTX = 8192.0
NORM_EPS = 1e-5
NEG_BIG = -1e30
EXP_SCALE = HEAD_DIM ** -0.5 * math.log2(math.e)

KC = 512
NB = 2048
N1 = 6
K_SLOT = 4
N2 = 9
BLOCKS_N = HALF // NB
Q_TRIPS = MODEL // (2 * KC)
O_CHUNKS = HEADS * HEAD_DIM // KC
O_WIDE = O_CHUNKS - 1
O_SLOTS = BLOCKS_N * O_WIDE
D_CHUNKS = FF // KC
D_OWN = D_CHUNKS // 2
D_REST = D_CHUNKS - D_OWN
D_FIRST = D_OWN * BLOCKS_N
D_SLOTS = D_CHUNKS * BLOCKS_N
D_EXTRA = N1
G_SLOTS = MODEL // KC
G_TRIPS = G_SLOTS // 2
BC = 2 * KC
BP = HALF // BC
XP = 4
PIECES_PER_SLOT = FFQ // LANES
KV_PIECES = MODEL // KC
KV_UNROLL = 8
HOOK_B, HOOK_C = 0, 10
PRE = 3
QL = 512
SCORE_BUFS = (0, 2 * QL)
NEAR = 6
STEPS = 18
DELIVER = 4096
NEIGHBOURS = (('x', 1), ('x', 3), ('y', 1), ('y', 3))
GROUPS = range(len(NEIGHBOURS))
GROUP = PAIR // len(NEIGHBOURS)

MESH = pl.DeviceIdType.MESH
F32 = jnp.float32
BF16 = jnp.bfloat16
BLOCKS = (((0, 1), 0, 'yzx'), ((1, 1), 0, 'zxy'), ((0, 2), 1, 'xyz'))
OWN = (0, 0, 0)
SENDS = ((OWN, 0), (OWN, 1), (OWN, 2), ((1, 0, 0), 1), ((1, 0, 0), 2), ((0, 1, 0), 2), ((1, 1, 0), 2))
ROUNDS = ((0, 1, 2), (3, 4, 5), (6,))
STEPS_ALONG = (1, 2, 3)


def dot(a, b):
    return jnp.dot(a, b, preferred_element_type=F32)


def span(first, count=LANES):
    return pl.ds(pl.multiple_of(first, LANES), count)


def iota(rows, cols, dim):
    return lax.broadcasted_iota(jnp.int32, (rows, cols), dim)


def rope_tables(pos):
    lane = iota(SUBLANES, HEAD_DIM, 1)
    j = lax.rem(lane, HEAD_DIM // 2).astype(F32)
    inv_freq = jnp.exp(j * (-2.0 / HEAD_DIM * math.log(ROPE_THETA)))
    wavelen = (2.0 * math.pi) / inv_freq
    smooth = jnp.clip((ORIG_CTX / wavelen - LOW_FREQ) / (HIGH_FREQ - LOW_FREQ), 0.0, 1.0)
    freq = ((1.0 - smooth) * inv_freq / ROPE_FACTOR + smooth * inv_freq)[:1]
    angle = pos * freq
    sign = jnp.where(lane[:1] < HEAD_DIM // 2, -1.0, 1.0)
    return jnp.cos(angle), jnp.sin(angle) * sign


def rope(t, cos_t, sin_t):
    return t * cos_t + pltpu.roll(t, HEAD_DIM // 2, 1) * sin_t


def layer_kernel(x_hbm, pos_ref, ag_ref, wq, wk, wv, wo, wo_rows, mg_ref, wg, wu, wd,
                 z_hbm, k_out, v_out,
                 x128, bbuf, w1, w2, acc, gacc, qt, ml, mx, obuf, mbuf, mst, st, ss, kst, gains,
                 xl_sem, xs_sem, xr_sem, sts_sem, str_sem, kvw_sem, w1_sem, w2_sem, gs_sem, gr_sem, fs_sem, fr_sem,
                 os_sem, or_sem, sss_sem, ssr_sem, bs_sem, br_sem, ns_sem, nr_sem, ms_sem, mr_sem, nms_sem, nmr_sem,
                 zl_sem, zs_sem, zr_sem, ko_sem, spare_sem, free_sem):
    me = lax.axis_index('cp')
    core = lax.rem(me, 2)
    chip = lax.div(me, 2)
    coords = {'x': lax.rem(chip, SIDE), 'y': lax.rem(lax.div(chip, SIDE), SIDE), 'z': lax.div(chip, SIDE * SIDE)}
    cx, cy, cz = coords['x'], coords['y'], coords['z']
    other = 1 - core
    sib = me + other - core
    color = lax.rem(cx + cy + cz, 2)
    hidden = pl.multiple_of(color * FFH + core * FFQ, LANES)

    def peer(dim, k, to_core=core):
        c = dict(coords)
        c[dim] = lax.rem(c[dim] + k, SIDE)
        return ((c['z'] * SIDE + c['y']) * SIDE + c['x']) * 2 + to_core

    def remote(src, dst, s, r, dev):
        return pltpu.make_async_remote_copy(src, dst, s, r, device_id={'cp': dev}, device_id_type=MESH)

    def to_sib(src, dst, s, r):
        return remote(src, dst, s, r, sib)

    own_rows = pl.ds(pl.multiple_of(core * ROWS, ROWS), ROWS)
    sib_rows = pl.ds(pl.multiple_of(other * ROWS, ROWS), ROWS)
    pair_rows = pl.ds(0, PAIR)
    own_half = pl.multiple_of(core * HALF, HALF)
    sib_half = pl.multiple_of(other * HALF, HALF)

    def w_rows(first):
        return pl.ds(lax.div(first, KC // 2), 2)

    def kv_dst(c, i):
        return w1.at[lax.div(c, PIECES_PER_SLOT), pl.ds(2 * i, 2), :, :, span(lax.rem(c, PIECES_PER_SLOT) * LANES)]

    def kv_copy(c, i):
        return pltpu.make_async_copy((wk, wv)[i].at[w_rows(c * KC)], kv_dst(c, i), kvw_sem.at[i, c])

    def o_chunk(u):
        return lax.rem(u + 2 * core, O_CHUNKS)

    def o_spare(n, h):
        rows = pl.ds(o_chunk(O_WIDE) * KC + h * PAIR * 2, PAIR * 2)
        return pltpu.make_async_copy(wo_rows.at[rows, span(own_half + n * NB, NB)], bbuf.at[:, span((2 * n + h) * NB, NB)], spare_sem.at[n, h])

    def d_place(i):
        first = i < D_FIRST
        n = jnp.where(first, lax.rem(i, BLOCKS_N), lax.div(i - D_FIRST, D_REST))
        return n, jnp.where(first, lax.div(i, BLOCKS_N), D_OWN + lax.rem(i - D_FIRST, D_REST))

    def d_chunk(kk):
        mine = color * D_REST + jnp.where(core == 0, kk, D_OWN - 1 - kk)
        return jnp.where(kk < D_OWN, mine, jnp.where(kk == D_OWN, D_OWN, (other_color * D_REST) + kk - D_REST))

    other_color = 1 - color

    def w2_start(n):
        slot = lax.rem(n, N2)

        @pl.when(n < Q_TRIPS)
        def _():
            for h in range(2):
                src = wq.at[w_rows(n * (2 * KC) + h * KC), :, :, span(core * QCOLS, QCOLS)]
                pltpu.make_async_copy(src, w2.at[slot, :, :, :, pl.ds(h * QCOLS, QCOLS)], w2_sem.at[slot]).start()

        @pl.when((n >= Q_TRIPS) & (n < Q_TRIPS + O_SLOTS))
        def _():
            i = n - Q_TRIPS
            src = wo.at[w_rows(o_chunk(lax.rem(i, O_WIDE)) * KC), :, :, span(own_half + lax.div(i, O_WIDE) * NB, NB)]
            pltpu.make_async_copy(src, w2.at[slot], w2_sem.at[slot]).start()

        @pl.when((n >= Q_TRIPS + O_SLOTS) & (n < Q_TRIPS + O_SLOTS + D_SLOTS - D_EXTRA))
        def _():
            i = n - (Q_TRIPS + O_SLOTS)
            block, kk = d_place(jnp.where(i < N2, i, i + D_EXTRA))
            src = wd.at[w_rows(d_chunk(kk) * KC), :, :, span(own_half + block * NB, NB)]
            pltpu.make_async_copy(src, w2.at[slot], w2_sem.at[slot]).start()

    def w2_wait(n):
        slot = lax.rem(n, N2)
        pltpu.make_async_copy(wo.at[w_rows(0), :, :, span(0, NB)], w2.at[slot], w2_sem.at[slot]).wait()
        return slot

    def wide(slot):
        return w2[slot].reshape(KC, NB)

    def g_cols(t):
        return pl.multiple_of(jnp.where(t < BP, own_half, sib_half) + lax.rem(t, BP) * BC, BC)

    def w1_start(n):
        slot = lax.rem(n, N1)

        @pl.when(n < G_SLOTS)
        def _():
            for i, w in enumerate((wg, wu)):
                src = w.at[w_rows(g_cols(lax.div(n, 2)) + lax.rem(n, 2) * KC), :, :, span(hidden, FFQ)]
                pltpu.make_async_copy(src, w1.at[slot, pl.ds(2 * i, 2)], w1_sem.at[slot]).start()

        @pl.when(n >= G_SLOTS)
        def _():
            block, kk = d_place(n - G_SLOTS + N2)
            for h in range(2):
                src = wd.at[w_rows(d_chunk(kk) * KC), :, :, span(own_half + block * NB + h * BC, BC)]
                pltpu.make_async_copy(src, w1.at[slot, pl.ds(2 * h, 2), :, :, span(0, BC)], w1_sem.at[slot]).start()

    def w1_wait(n):
        slot = lax.rem(n, N1)
        pltpu.make_async_copy(wg.at[pl.ds(0, SIDE), :, :, span(0, FFQ)], w1.at[slot], w1_sem.at[slot]).wait()
        return slot

    def w1_wait_down(n):
        slot = lax.rem(n, N1)
        pltpu.make_async_copy(wd.at[pl.ds(0, SIDE), :, :, span(0, BC)], w1.at[slot, :, :, :, span(0, BC)], w1_sem.at[slot]).wait()
        return slot

    x_local = pltpu.make_async_copy(x_hbm, x128.at[own_rows, :], xl_sem)
    x_local.start()
    barrier = pltpu.get_barrier_semaphore()
    greeted = [sib] + [peer(dim, k) for dim in 'xyz' for k in STEPS_ALONG] + [peer(dim, k, other) for dim, k in NEIGHBOURS]
    for dev in greeted:
        pl.semaphore_signal(barrier, device_id={'cp': dev}, device_id_type=MESH)

    @pl.loop(0, KV_PIECES)
    def _(c):
        for i in range(2):
            kv_copy(c, i).start()

    def x_copy(i):
        cols = span(i * (MODEL // XP), MODEL // XP)
        return to_sib(x_hbm.at[:, cols], x128.at[own_rows, cols], xs_sem.at[i], xr_sem.at[i])

    eye = iota(ROWS, ROWS, 0) == iota(ROWS, ROWS, 1)
    pos_own = jnp.sum(jnp.where(eye, jnp.broadcast_to(pos_ref[...].astype(F32), (ROWS, ROWS)), 0.0), axis=1, keepdims=True)
    cos_own, sin_own = rope_tables(pos_own)
    gains[0] = ag_ref[...].astype(F32)
    gains[1] = mg_ref[...].astype(F32)

    x_local.wait()

    def square_sum(i, part):
        for u in range(SUBLANES):
            v = x128[own_rows, span(i * BC + u * LANES)].astype(F32)
            part = part + v * v
        return part

    part = lax.fori_loop(0, MODEL // BC, square_sum, jnp.zeros((ROWS, LANES), F32))
    inv_own = lax.rsqrt(jnp.sum(part, axis=1, keepdims=True) / MODEL + NORM_EPS)
    pl.semaphore_wait(barrier, len(greeted))
    for i in range(XP):
        x_copy(i).start()
    st[core] = jnp.where(iota(ROWS, LANES, 1) == 0, inv_own, pos_own)
    st_copy = to_sib(st.at[core], st.at[core], sts_sem, str_sem)
    st_copy.start()

    def normalize(rows, inv, lo, hi):
        @pl.loop(lo, hi)
        def _(i):
            for u in range(SUBLANES):
                tile = i * SUBLANES + u
                cols = span(tile * LANES)
                bbuf[rows, cols] = (x128[rows, cols].astype(F32) * inv * gains[0, pl.ds(tile, 1), :]).astype(BF16)

    normalize(own_rows, inv_own, 0, MODEL // BC)

    @pl.loop(0, N2)
    def _(n):
        w2_start(n)

    def kv_trip(i, total):
        places = [i * KV_UNROLL + u for u in range(KV_UNROLL)]
        for c in places:
            for j in range(2):
                kv_copy(c, j).wait()
        for c in places:
            w = jnp.concatenate([kv_dst(c, j)[...].reshape(KC, LANES) for j in range(2)], axis=1)
            total = total + dot(bbuf[own_rows, span(c * KC, KC)], w)
        return total

    kv_raw = lax.fori_loop(0, KV_PIECES // KV_UNROLL, kv_trip, jnp.zeros((ROWS, 2 * LANES), F32))
    r0 = (pl.multiple_of(core * CHUNK, CHUNK), pl.multiple_of(other * CHUNK, CHUNK))
    stores = []
    for i, (t, out) in enumerate(((rope(kv_raw[:, :LANES], cos_own, sin_own), k_out), (kv_raw[:, LANES:], v_out))):
        t = t.astype(BF16)
        w1[K_SLOT + i, 0, 0, pl.ds(r0[0], CHUNK), :LANES] = t[:CHUNK]
        w1[K_SLOT + i, 0, 0, pl.ds(r0[1], CHUNK), span(SIDE * LANES)] = t[CHUNK:]
        kst[i] = t
        stores.append(pltpu.make_async_copy(kst.at[i], out, ko_sem.at[i]))
        stores[i].start()

    def region(b, spec, dim=None, place=None, rows=0):
        slots, half, dims = BLOCKS[b]

        def at(d):
            first, count = (place, 1) if d == dim else (1, SIDE - 1) if spec[dims.index(d)] else (0, 1)
            return first, count

        first, count = at('z')
        lanes = pl.ds((half * SIDE + first) * LANES, count * LANES)
        rows = pl.ds(r0[half if rows == 0 else 1 - half], CHUNK)
        return w1.at[pl.ds(K_SLOT + slots[0], slots[1]), pl.ds(*at('y')), pl.ds(*at('x')), rows, lanes]

    def gather_copy(b, n, k):
        spec, along = SENDS[n]
        dim = BLOCKS[b][2][along]
        return remote(region(b, spec), region(b, spec, dim, SIDE - k), gs_sem.at[b, n, k - 1], gr_sem.at[b, n, k - 1], peer(dim, k))

    def forward(b, n, k, rows=0):
        spec, along = SENDS[n]
        part = region(b, spec, BLOCKS[b][2][along], SIDE - k, rows)
        return to_sib(part, part, fs_sem.at[b, n, k - 1], fr_sem.at[b, n, k - 1])

    def own_forward(b, rows=0):
        part = region(b, OWN, rows=rows)
        return to_sib(part, part, fs_sem.at[b, len(SENDS), 0], fr_sem.at[b, len(SENDS), 0])

    def each(sends, side, action):
        for n in sends:
            for b in range(len(BLOCKS)):
                for k in STEPS_ALONG:
                    if BLOCKS[b][1] == 1 and BLOCKS[b][2][SENDS[n][1]] == 'z':
                        pl.when(cz + k >= SIDE if side == 'send' else cz < k)(functools.partial(action, b, n, k))
                    else:
                        action(b, n, k)

    def send(b, n, k):
        gather_copy(b, n, k).start()

    def sent(b, n, k):
        gather_copy(b, n, k).wait_send()

    def receive(b, n, k):
        gather_copy(b, n, k).wait_recv()

    def pass_on(b, n, k):
        forward(b, n, k).start()

    def receive_pass_on(b, n, k):
        receive(b, n, k)
        pass_on(b, n, k)

    def passed(b, n, k):
        forward(b, n, k).wait_send()
        forward(b, n, k, 1).wait_recv()

    each(ROUNDS[0], 'send', send)
    for b in range(len(BLOCKS)):
        own_forward(b).start()

    def second_round():
        each(ROUNDS[0][:2], 'recv', receive)
        each(ROUNDS[1], 'send', send)
        each(ROUNDS[0][:2], 'recv', pass_on)
        each(ROUNDS[0][2:], 'recv', receive_pass_on)

    def third_round():
        each(ROUNDS[1][:1], 'recv', receive)
        each(ROUNDS[2], 'send', send)
        each(ROUNDS[1][:1], 'recv', pass_on)

    def own_plane_there():
        each(ROUNDS[1][1:], 'recv', receive_pass_on)
        for b in range(len(BLOCKS)):
            own_forward(b).wait_send()
            own_forward(b, 1).wait_recv()
        each(ROUNDS[0] + ROUNDS[1], 'recv', passed)

    def all_there():
        each(ROUNDS[2], 'recv', receive_pass_on)
        each(ROUNDS[2], 'recv', passed)

    st_copy.wait()
    inv_sib = st[other][:, :1]
    for i in range(XP):
        x_copy(i).wait()
        normalize(sib_rows, inv_sib, i * XP, (i + 1) * XP)

    acc[0] = jnp.zeros((PAIR, NB), F32)

    @pl.loop(0, Q_TRIPS)
    def _(i):
        pl.when(i == HOOK_B)(second_round)
        pl.when(i == HOOK_C)(third_round)
        w = wide(w2_wait(i))
        acc[0, :, :QCOLS] += (dot(bbuf[pair_rows, span(i * BC, KC)], w[:, :QCOLS])
                              + dot(bbuf[pair_rows, span(i * BC + KC, KC)], w[:, QCOLS:]))
        w2_start(i + N2)

    for n in range(BLOCKS_N):
        for h in range(2):
            o_spare(n, h).start()

    @pl.loop(0, K_SLOT)
    def _(n):
        w1_start(n)

    pos_all = jnp.concatenate([st[i][:, 1:2] for i in range(2)], axis=0)
    cos_t, sin_t = rope_tables(pos_all)
    EARLY = (slice(0, CHUNK), slice(ROWS, ROWS + CHUNK))
    LATE = (slice(ROWS + CHUNK, PAIR), slice(CHUNK, ROWS))
    for hp in range(PAIR_HEADS):
        q = [rope(acc[0, :, span(h * LANES)], cos_t, sin_t) for h in (2 * hp, 2 * hp + 1)]
        for half, rows in enumerate((EARLY, LATE)):
            qt[half, :, span(hp * LANES)] = jnp.concatenate([v[r] for v in q for r in rows], axis=0).T.astype(BF16)

    own_plane_there()
    ml[:, 0] = jnp.full((2, SUBLANES, QL), NEG_BIG, F32)
    ml[:, 1] = jnp.zeros((2, SUBLANES, QL), F32)
    acc[:2, :, :QL] = jnp.zeros((2, HEAD_DIM, QL), F32)
    row_of = iota(PAIR, LANES, 0)
    r64 = lax.rem(iota(PAIR, LANES, 1), ROWS)

    def row_positions(rows):
        src = jnp.where(r64 < CHUNK, r64 + rows[0].start, r64 + (rows[1].start - CHUNK))
        return jnp.sum(jnp.where(row_of == src, pos_all, 0.0), axis=0, keepdims=True).astype(jnp.int32)

    pos_e, pos_l = row_positions(EARLY), row_positions(LATE)

    def natural(late, c):
        return jnp.where(late, SEQ - ROWS * (c + 1), ROWS * c)

    def step(s):
        near = s < NEAR
        r = lax.div(s - NEAR, 2)
        late_q = jnp.where(near, s >= 2, r >= cz)
        late_k = jnp.where(near, lax.div(s, 2) == 1, late_q & (r < SIDE - 1))
        dz = jnp.where(near, 0, jnp.where(late_q, jnp.where(r < SIDE - 1, r - cz + 1, r - 2), SIDE - 1 - r))
        lanes = span((late_k.astype(jnp.int32) * SIDE + dz) * LANES)
        return late_q, late_k, dz, lax.rem(s, 2) * 2, lanes

    def product(s, buf):
        late_q, late_k, dz, dy, lanes = step(s)
        q = qt[late_q.astype(jnp.int32)]
        row_nat = natural(late_q, chip) + r64[:1]
        row_first = row_nat - jnp.where(late_q, pos_l, pos_e)
        plane = lax.rem(cz + dz, SIDE) * SIDE
        u = iota(ROWS, 1, 0)
        tops = [jnp.full((SUBLANES, LANES), NEG_BIG, F32)] * SIDE
        for part in range(2):
            keys = w1[K_SLOT, dy + part, :, :, lanes].reshape(SIDE * ROWS, LANES)
            row_y = (plane + lax.rem(cy + dy + part, SIDE)) * SIDE
            scores = dot(keys, q)
            for i in range(SIDE):
                key_nat = natural(late_k, row_y + lax.rem(cx + i, SIDE)) + u
                visible = (key_nat >= row_first) & (key_nat <= row_nat)
                rows = slice(i * ROWS, (i + 1) * ROWS)
                for l in range(SIDE):
                    tile = jnp.where(visible, scores[rows, l * LANES:(l + 1) * LANES], NEG_BIG)
                    gacc[rows, span(SCORE_BUFS[buf] + part * QL + l * LANES)] = tile
                    for r in range(0, ROWS, SUBLANES):
                        tops[l] = jnp.maximum(tops[l], tile[r:r + SUBLANES])
        mx[buf] = jnp.concatenate(tops, axis=1)

    def soften(s, buf):
        late_q, _, _, dy, lanes = step(s)
        qh = late_q.astype(jnp.int32)
        m_old = ml[qh, 0, :1]
        m_new = jnp.maximum(m_old, jnp.max(mx[buf], axis=0, keepdims=True))
        shift = m_new * EXP_SCALE
        p = jnp.concatenate([jnp.exp2(gacc[:, span(SCORE_BUFS[buf] + i * QL, QL)] * EXP_SCALE - shift) for i in range(2)], axis=0)
        alpha = jnp.exp2((m_old - m_new) * EXP_SCALE)
        ml[qh, 0, :1] = m_new
        ml[qh, 1, :1] = ml[qh, 1, :1] * alpha + jnp.sum(p, axis=0, keepdims=True)
        vals = w1[K_SLOT + 1, pl.ds(dy, 2), :, :, lanes].reshape(2 * SIDE * ROWS, LANES)
        pv = lax.dot_general(vals, p.astype(BF16), (((0,), (0,)), ((), ())), preferred_element_type=F32)
        acc[qh, :, :QL] = acc[qh, :, :QL] * alpha + pv

    product(0, 0)

    @pl.loop(0, STEPS // 2)
    def _(i):
        @pl.when(i == NEAR // 2)
        def _():
            all_there()
            product(NEAR, 0)

        product(2 * i + 1, 1)
        soften(2 * i, 0)
        product(jnp.where((i == NEAR // 2 - 1) | (i == STEPS // 2 - 1), 0, 2 * i + 2), 0)
        soften(2 * i + 1, 1)

    for hp in range(PAIR_HEADS):
        for half, rows in enumerate((EARLY, LATE)):
            o = (acc[half, :, span(hp * LANES)] / ml[half, 1, :1, span(hp * LANES)]).T.astype(BF16)
            for u in range(2):
                for i, r in enumerate(rows):
                    obuf[core, r, span((2 * hp + u) * LANES)] = o[ROWS * u + CHUNK * i:ROWS * u + CHUNK * (i + 1)]
    o_copy = to_sib(obuf.at[core], obuf.at[core], os_sem, or_sem)
    o_copy.start()
    each(range(len(SENDS)), 'send', sent)
    for n in range(K_SLOT, N1):
        w1_start(n)

    def o_part(n, own):
        group = core if own else other
        places = range(2) if own else range(2, O_WIDE)
        slots = [w2_wait(Q_TRIPS + O_WIDE * n + u) for u in places]

        def part(cols):
            terms = [dot(obuf[group, :, u % 2 * KC:(u % 2 + 1) * KC], w2[s, :, :, :, cols].reshape(KC, QL)) for u, s in zip(places, slots)]
            if not own:
                for h in range(2):
                    w = bbuf[:, span((2 * n + h) * NB + cols.start, QL)]
                    terms.append(dot(obuf[group, :, span(KC + h * PAIR * 2, PAIR * 2)], w))
            return sum(terms)

        return part

    def o_block(n, parts):
        total = jnp.zeros((PAIR, LANES), F32)
        for h in range(2):
            o_spare(n, h).wait()
        for b in range(0, NB, QL):
            out = sum(p(slice(b, b + QL)) for p in parts)
            cols = span(own_half + n * NB + b, QL)
            h = (x128[:, cols].astype(F32) + out).astype(BF16)
            x128[:, cols] = h
            hf = h.astype(F32)
            for u in range(0, QL, LANES):
                total = total + hf[:, u:u + LANES] * hf[:, u:u + LANES]
        ss[core] += total
        for u in range(O_WIDE):
            w2_start(Q_TRIPS + O_WIDE * n + u + N2)

    ss[core] = jnp.zeros((PAIR, LANES), F32)
    first = o_part(0, True)
    for b in range(0, NB, QL):
        acc[0, :, b:b + QL] = first(slice(b, b + QL))
    o_copy.wait()
    o_block(0, [lambda cols: acc[0, :, cols], o_part(0, False)])

    @pl.loop(1, BLOCKS_N)
    def _(n):
        o_block(n, [o_part(n, True), o_part(n, False)])

    for dim, k in NEIGHBOURS:
        for c in range(2):
            pl.semaphore_signal(free_sem, device_id={'cp': peer(dim, SIDE - k, c)}, device_id_type=MESH)
    ss_copy = to_sib(ss.at[core], ss.at[core], sss_sem, ssr_sem)
    ss_copy.start()
    gacc[...] = jnp.zeros_like(gacc)
    ss_copy.wait()
    inv_h = lax.rsqrt(jnp.sum(ss[0] + ss[1], axis=1, keepdims=True) / MODEL + NORM_EPS)

    def b_copy(i, half=own_half):
        part = bbuf.at[pair_rows, span(half + i * BC, BC)]
        return to_sib(part, part, bs_sem.at[i], br_sem.at[i])

    def n_copy(cross, i, g):
        dim, k = NEIGHBOURS[g]
        cols = span(own_half + i * BC, BC)
        return remote(bbuf.at[pl.ds(g * GROUP, GROUP), cols], bbuf.at[pl.ds(PAIR + g * GROUP, GROUP), cols],
                      ns_sem.at[cross, i, g], nr_sem.at[cross, i, g], peer(dim, k, other if cross else core))

    def n_arrival(cross, i, g):
        dim, k = NEIGHBOURS[g]
        dst = bbuf.at[pl.ds(PAIR + g * GROUP, GROUP), span((sib_half if cross else own_half) + i * BC, BC)]
        return remote(dst, dst, ns_sem.at[cross, i, g], nr_sem.at[cross, i, g], peer(dim, SIDE - k, other if cross else core))

    pl.semaphore_wait(free_sem, 2 * len(NEIGHBOURS))

    @pl.loop(0, BP)
    def _(i):
        for j in range(BC // LANES):
            tile = core * (HALF // LANES) + i * (BC // LANES) + j
            cols = span(tile * LANES)
            bbuf[pair_rows, cols] = (x128[:, cols].astype(F32) * inv_h * gains[1, pl.ds(tile, 1), :]).astype(BF16)
        for g in GROUPS:
            n_copy(0, i, g).start()
        b_copy(i).start()

    @pl.loop(0, BP)
    def _(i):
        for g in GROUPS:
            n_copy(1, i, g).start()

    def gate_up(rows, t, slots):
        parts = [(bbuf[rows, span(g_cols(t) + u * KC, KC)], s) for u, s in enumerate(slots)]

        def block(i, cols):
            return [w1[s, 2 * i:2 * i + 2, :, :, cols].reshape(KC, cols.stop - cols.start) for _, s in parts]

        def product_of(weights):
            return sum(dot(a, w) for (a, _), w in zip(parts, weights))

        for i in range(2):
            for b in range(0, FFQ - LANES, QL):
                gacc[rows, i * FFQ + b:i * FFQ + b + QL] += product_of(block(i, slice(b, b + QL)))
        last = slice(FFQ - LANES, FFQ)
        pair = product_of([jnp.concatenate(w, axis=1) for w in zip(block(0, last), block(1, last))])
        gacc[rows, last] += pair[:, :LANES]
        gacc[rows, 2 * FFQ - LANES:] += pair[:, LANES:]

    def refill(t):
        for u in range(2):
            w1_start(2 * t + u + N1)

    @pl.loop(0, PRE)
    def _(t):
        gate_up(slice(0, PAIR), t, [w1_wait(2 * t + u) for u in range(2)])

    @pl.loop(0, PRE)
    def _(t):
        for g in GROUPS:
            n_arrival(0, t, g).wait_recv()
        gate_up(slice(PAIR, 2 * PAIR), t, [2 * t + u for u in range(2)])
        refill(t)

    @pl.loop(PRE, G_TRIPS)
    def _(t):
        @pl.when(t < BP)
        def _():
            for g in GROUPS:
                n_arrival(0, t, g).wait_recv()

        @pl.when(t >= BP)
        def _():
            b_copy(t - BP, sib_half).wait_recv()
            for g in GROUPS:
                n_arrival(1, t - BP, g).wait_recv()

        gate_up(slice(0, 2 * PAIR), t, [w1_wait(2 * t + u) for u in range(2)])
        refill(t)

    def gated(rows, j):
        g = gacc[rows, span(j * LANES)]
        return (g * (1.0 / (1.0 + jnp.exp(-g))) * gacc[rows, span(FFQ + j * LANES)]).astype(BF16)

    @pl.loop(0, FFQ // LANES)
    def _(j):
        mst[:, span(j * LANES)] = gated(pl.ds(PAIR, PAIR), j)

    def nm_copy(cross, g):
        dim, k = NEIGHBOURS[g]
        return remote(mst.at[pl.ds(g * GROUP, GROUP), :], mbuf.at[pl.ds(g * GROUP, GROUP), span(hidden, FFQ)],
                      nms_sem.at[cross, g], nmr_sem.at[cross, g], peer(dim, SIDE - k, other if cross else core))

    def nm_arrival(cross, g):
        dim, k = NEIGHBOURS[g]
        dst = mbuf.at[pl.ds(g * GROUP, GROUP), span(other_color * FFH + (other if cross else core) * FFQ, FFQ)]
        return remote(dst, dst, nms_sem.at[cross, g], nmr_sem.at[cross, g], peer(dim, k, other if cross else core))

    for cross in range(2):
        for g in GROUPS:
            nm_copy(cross, g).start()

    @pl.loop(0, FFQ // LANES)
    def _(j):
        mbuf[:, span(hidden + j * LANES)] = gated(pair_rows, j)

    def m_copy(of_core):
        part = mbuf.at[:, span(color * FFH + of_core * FFQ, FFQ)]
        return to_sib(part, part, ms_sem, mr_sem)

    m_copy(core).start()

    acc[...] = jnp.zeros_like(acc)

    @pl.loop(0, BP)
    def _(i):
        b_copy(i).wait_send()
        for cross in range(2):
            for g in GROUPS:
                n_copy(cross, i, g).wait_send()

    def z_cols(n, half=own_half):
        return span(half + n * NB, NB)

    def z_local(n):
        return pltpu.make_async_copy(bbuf.at[own_rows, z_cols(n)], z_hbm.at[:, z_cols(n)], zl_sem.at[n])

    def z_remote(n, half=own_half):
        return to_sib(bbuf.at[sib_rows, z_cols(n)], z_hbm.at[:, z_cols(n, half)], zs_sem.at[n], zr_sem.at[n])

    def down(i, weight):
        n, kk = d_place(i)
        a = mbuf[:, span(d_chunk(kk) * KC, KC)]
        acc[n] += dot(a, weight)

    @pl.loop(0, N2)
    def _(i):
        @pl.when(i == 2 * BLOCKS_N)
        def _():
            m_copy(core).wait_send()
            m_copy(other).wait_recv()

        down(i, wide(w2_wait(Q_TRIPS + O_SLOTS + i)))
        w2_start(Q_TRIPS + O_SLOTS + i + N2)

    @pl.loop(0, D_EXTRA)
    def _(i):
        slot = w1_wait_down(G_SLOTS + i)
        down(i + N2, jnp.concatenate([w1[slot, 2 * h:2 * h + 2, :, :, :BC].reshape(KC, BC) for h in range(2)], axis=1))

    @pl.loop(N2, D_SLOTS - D_EXTRA)
    def _(j):
        i = j + D_EXTRA

        @pl.when(i == D_FIRST)
        def _():
            for cross in range(2):
                for g in GROUPS:
                    nm_arrival(cross, g).wait_recv()

        down(i, wide(w2_wait(Q_TRIPS + O_SLOTS + j)))
        w2_start(Q_TRIPS + O_SLOTS + j + N2)
        n, kk = d_place(i)

        @pl.when(kk == D_CHUNKS - 1)
        def _():
            @pl.loop(0, NB // QL)
            def _(b):
                cols = span(own_half + n * NB + b * QL, QL)
                bbuf[pair_rows, cols] = (x128[:, cols].astype(F32) + acc[n, :, span(b * QL, QL)]).astype(BF16)

            z_local(n).start()
            z_remote(n).start()

    for n in range(BLOCKS_N):
        z_local(n).wait()
        z_remote(n).wait_send()
        z_remote(n, sib_half).wait_recv()
    for cross in range(2):
        for g in GROUPS:
            nm_copy(cross, g).wait_send()
    for s in stores:
        s.wait()


def deliver_kernel(z_in, k_in, v_in, z_out, k_out, v_out, zb, kb, in_sem, out_sem):
    moves = [(k_in, kb.at[0], k_out), (v_in, kb.at[1], v_out)]
    for first in range(0, MODEL, DELIVER):
        cols = span(first, DELIVER)
        moves.append((z_in.at[:, cols], zb.at[:, cols], z_out.at[:, cols]))
    moves = [(pltpu.make_async_copy(src, mid, in_sem.at[i]), pltpu.make_async_copy(mid, dst, out_sem.at[i])) for i, (src, mid, dst) in enumerate(moves)]
    for come, _ in moves:
        come.start()
    for come, go in moves:
        come.wait()
        go.start()
    for _, go in moves:
        go.wait()


def solution(mesh):
    def device_fn(x_loc, seg_loc, pos_loc, attn_gain, w_q, w_k, w_v, w_o, mlp_gain, w_gate, w_up, w_down):
        any_space = pl.BlockSpec(memory_space=pl.ANY)
        vmem = pl.BlockSpec(memory_space=pltpu.VMEM)

        def blocks(w):
            return w.reshape(-1, SIDE, ROWS, w.shape[1])

        def gain(g):
            return g.reshape(-1, LANES)

        z_shape, k_shape = (jax.ShapeDtypeStruct((ROWS, n), BF16) for n in (MODEL, HEAD_DIM))
        outs = (z_shape, k_shape, k_shape)
        f32_buffers = ((BLOCKS_N, PAIR, NB), (2 * PAIR, 2 * FFQ))
        stats = ((2, 2, SUBLANES, QL), (2, SUBLANES, QL))
        sems = {
            'xl': (), 'xs': (XP,), 'xr': (XP,), 'sts': (), 'str': (), 'kvw': (2, KV_PIECES), 'w1': (N1,), 'w2': (N2,),
            'gs': (len(BLOCKS), len(SENDS), len(STEPS_ALONG)), 'gr': (len(BLOCKS), len(SENDS), len(STEPS_ALONG)),
            'fs': (len(BLOCKS), len(SENDS) + 1, len(STEPS_ALONG)), 'fr': (len(BLOCKS), len(SENDS) + 1, len(STEPS_ALONG)),
            'os': (), 'or': (), 'sss': (), 'ssr': (), 'bs': (BP,), 'br': (BP,), 'ns': (2, BP, len(GROUPS)), 'nr': (2, BP, len(GROUPS)),
            'ms': (), 'mr': (), 'nms': (2, len(GROUPS)), 'nmr': (2, len(GROUPS)), 'zl': (BLOCKS_N,), 'zs': (BLOCKS_N,), 'zr': (BLOCKS_N,), 'ko': (2,), 'spare': (BLOCKS_N, 2),
        }

        def dma(shape):
            return pltpu.SemaphoreType.DMA(shape) if shape else pltpu.SemaphoreType.DMA

        results = pl.pallas_call(
            layer_kernel,
            out_shape=outs,
            in_specs=[any_space, vmem, vmem, any_space, any_space, any_space, any_space, any_space, vmem, any_space, any_space, any_space],
            out_specs=(any_space,) * len(outs),
            scratch_shapes=[
                pltpu.VMEM((PAIR, MODEL), BF16),
                pltpu.VMEM((2 * PAIR, MODEL), BF16),
                pltpu.VMEM((N1, SIDE, SIDE, ROWS, FFQ), BF16),
                pltpu.VMEM((N2, 2, SIDE, ROWS, NB), BF16),
                *(pltpu.VMEM(s, F32) for s in f32_buffers),
                pltpu.VMEM((2, HEAD_DIM, QL), BF16),
                *(pltpu.VMEM(s, F32) for s in stats),
                pltpu.VMEM((2, PAIR, QCOLS), BF16),
                pltpu.VMEM((PAIR, FF), BF16),
                pltpu.VMEM((PAIR, FFQ), BF16),
                pltpu.VMEM((2, ROWS, LANES), F32),
                pltpu.VMEM((2, PAIR, LANES), F32),
                pltpu.VMEM((2, ROWS, LANES), BF16),
                pltpu.VMEM((2, LANES, LANES), F32),
                *(dma(s) for s in sems.values()),
                pltpu.SemaphoreType.REGULAR,
            ],
            compiler_params=pltpu.CompilerParams(collective_id=0, has_side_effects=True, vmem_limit_bytes=67043328),
            name='layer',
        )(x_loc[0], pos_loc.reshape(1, ROWS), gain(attn_gain), blocks(w_q), blocks(w_k), blocks(w_v), blocks(w_o), w_o, gain(mlp_gain),
          blocks(w_gate), blocks(w_up), blocks(w_down))
        moves = MODEL // DELIVER + 2
        z_rows, k_rows, v_rows = pl.pallas_call(
            deliver_kernel,
            out_shape=outs,
            in_specs=[any_space] * len(outs),
            out_specs=(any_space,) * len(outs),
            scratch_shapes=[pltpu.VMEM((ROWS, MODEL), BF16), pltpu.VMEM((2, ROWS, HEAD_DIM), BF16), dma((moves,)), dma((moves,))],
            compiler_params=pltpu.CompilerParams(vmem_limit_bytes=62914560),
            name='finish',
        )(*results)
        return z_rows[None], k_rows[:, None, :], v_rows[:, None, :]

    seq_spec = P(('dp', 'cp'))
    rows_spec, cache_spec = P('dp', 'cp', None), P(('dp', 'cp'), None, None)
    return jax.shard_map(device_fn, mesh=mesh, in_specs=(rows_spec, seq_spec, seq_spec) + (P(),) * 9, out_specs=(rows_spec, cache_spec, cache_spec), check_vma=False)
```

time: 1610 us -> 118 us (0.07)
  waiting for transfers between devices: 1050 us -> 0 us
  matrix products: 368 us -> 0 us
  Pallas kernels: 0 us -> 118 us
  local copies, waits for them, and re-layouts: 84.3 us -> 0 us
  starting transfers between devices: 47.5 us -> 0 us
  other arithmetic: 33 us -> 0 us
  loops' own time: 18.4 us -> 0 us
    ppermute x508 -> x0, waiting for transfers between devices: 1050 us -> none  [remote_step(): held = lax.ppermute(held, 'cp', shift)]
    dot_general x263 -> x0, matrix products: 368 us -> none  [the longest x1 69.9 us: finish_rows(): jnp.dot(hidden, w_down, preferred_element_type=jnp.float32)]
    pallas_call x0 -> x2, Pallas kernels: none -> 118 us  [the longest x1 115 us: device_fn(): pl.pallas_call(layer_kernel, out_shape=outs, in_specs=[any_space, vmem, v...]
    dot_general x1 -> x0, local copies, waits for them, and re-layouts: 81.7 us -> none  [project_rows(): jnp.dot(normed, w_q, preferred_element_type=jnp.float32)]
    ppermute x508 -> x0, starting transfers between devices: 47.5 us -> none  [remote_step(): held = lax.ppermute(held, 'cp', shift)]
    another operation x1 -> x0, loops' own time: 18.4 us -> none  [device_fn(): lax.fori_loop(0, cp_size - 1, remote_step, (state, (k_heads, v_heads, seg...]
    reduce_sum x129 -> x0, other arithmetic: 18.1 us -> none  [the longest x128 16 us: attend_block(): l_new = l_run * rescale + jnp.sum(prob_w, axis=-1)]
  transfers between devices with their start and end apart: 508 -> 0, of which waited for: 253 -> 0; matrix products, arithmetic and copies ran while one was open for 5% -> 0% of each run, Pallas kernels for 0% -> 0%
where the time goes in v2:
time: 118 us
  Pallas kernels  118 us (100%)
    pallas_call x1, Pallas kernels, device_fn(): pl.pallas_call(layer_kernel, out_shape=outs, in_specs=[any_space, vmem, v...  115 us
    pallas_call x1, Pallas kernels, device_fn(): pl.pallas_call(deliver_kernel, out_shape=outs, in_specs=[any_space] * len...  2.49 us

profile of v2, /device:TPU:1, one launch (start us, length us, event | category | flops | bytes accessed | tf_op | source)
XLA Modules:
  0.0 118.2 jit_solution(9029175224178749359)
XLA Ops:
  0.6 115.1 %layer.1 = (bf16[64,16384]{1,0:T(8,128)(2,1)}, bf16[64,128]{1,0:T(8,128)(2,1)}, bf16[64,128]{1,0:T(8,128)(2,1)}) custom-call(bf16[64,16384]{1,0:T(8,128)(2,1)} %bitcast.16, s32[1,64]{1,0:T(1,128)} %bitcast.19, bf16[128,128]{1,0:T(8,128)(2,1)} %bitcast.17, bf16[64,4,64,2048]{3,2,1,0:T(8,128)(2,1)} %bitcast.3.wq, bf16[64,4,64,128]{3,2,1,0:T(8,128)(2,1)} %bitcast.14, ...), custom_call_target="tpu_custom_call" | custom-call | tf_op jit(solution)/shard_map/layer/pallas_call | solution.py:782
  115.7 2.5 %finish.1 = (bf16[64,16384]{1,0:T(8,128)(2,1)}, bf16[64,128]{1,0:T(8,128)(2,1)}, bf16[64,128]{1,0:T(8,128)(2,1)}) custom-call(bf16[64,16384]{1,0:T(8,128)(2,1)} %get-tuple-element.9.z_in, bf16[64,128]{1,0:T(8,128)(2,1)} %get-tuple-element.10.k_in, bf16[64,128]{1,0:T(8,128)(2,1)} %get-tuple-element.11.v_in), custom_call_target="tpu_custom_call" | custom-call | tf_op jit(solution)/shard_map/finish/pallas_call | solution.py:810

commit v3 on v2

--- a/solution.py
+++ b/solution.py
@@ -13,6 +13,7 @@
 SIDE = 4
 MODEL = 16384
 HALF = MODEL // 2
+QUARTER = MODEL // 4
 HEADS = 16
 PAIR_HEADS = HEADS // 4
 HEAD_DIM = LANES
@@ -46,9 +47,11 @@
 D_CHUNKS = FF // KC
 D_OWN = D_CHUNKS // 2
 D_REST = D_CHUNKS - D_OWN
-D_FIRST = D_OWN * BLOCKS_N
-D_SLOTS = D_CHUNKS * BLOCKS_N
-D_EXTRA = N1
+D_BLOCKS = QUARTER // NB
+D_FIRST = D_OWN * D_BLOCKS
+D_SLOTS = D_CHUNKS * D_BLOCKS
+D_WIDE = tuple(range(8)) + (12,) + tuple(range(15, 23))
+D_NARROW = tuple(range(8, 12)) + (13, 14, 23, 24, 25)
 G_SLOTS = MODEL // KC
 G_TRIPS = G_SLOTS // 2
 BC = 2 * KC
@@ -57,8 +60,8 @@
 PIECES_PER_SLOT = FFQ // LANES
 KV_PIECES = MODEL // KC
 KV_UNROLL = 8
-HOOK_B, HOOK_C = 0, 10
-PRE = 3
+HOOK_B, HOOK_C = 0, 12
+PRE = 2
 QL = 512
 SCORE_BUFS = (0, 2 * QL)
 NEAR = 6
@@ -108,10 +111,10 @@
 
 def layer_kernel(x_hbm, pos_ref, ag_ref, wq, wk, wv, wo, wo_rows, mg_ref, wg, wu, wd,
                  z_hbm, k_out, v_out,
-                 x128, bbuf, w1, w2, acc, gacc, qt, ml, mx, obuf, mbuf, mst, st, ss, kst, gains,
+                 x128, bbuf, w1, w2, acc, gacc, qt, ml, mx, obuf, mbuf, st, ss, kst, gains,
                  xl_sem, xs_sem, xr_sem, sts_sem, str_sem, kvw_sem, w1_sem, w2_sem, gs_sem, gr_sem, fs_sem, fr_sem,
-                 os_sem, or_sem, sss_sem, ssr_sem, bs_sem, br_sem, ns_sem, nr_sem, ms_sem, mr_sem, nms_sem, nmr_sem,
-                 zl_sem, zs_sem, zr_sem, ko_sem, spare_sem, free_sem):
+                 os_sem, or_sem, sss_sem, ssr_sem, bs_sem, br_sem, ns_sem, nr_sem, ms_sem, mr_sem, nms_sem, nmr_sem, fms_sem, fmr_sem, hs_sem, hr_sem,
+                 za_sem, zb_sem, zl_sem, zs_sem, zr_sem, ko_sem, spare_sem, free_sem):
     me = lax.axis_index('cp')
     core = lax.rem(me, 2)
     chip = lax.div(me, 2)
@@ -136,8 +139,15 @@
     own_rows = pl.ds(pl.multiple_of(core * ROWS, ROWS), ROWS)
     sib_rows = pl.ds(pl.multiple_of(other * ROWS, ROWS), ROWS)
     pair_rows = pl.ds(0, PAIR)
-    own_half = pl.multiple_of(core * HALF, HALF)
-    sib_half = pl.multiple_of(other * HALF, HALF)
+
+    def col_of(c, v):
+        return lax.div(v, QUARTER) * HALF + c * QUARTER + lax.rem(v, QUARTER)
+
+    def own_col(v):
+        return col_of(core, v)
+
+    def sib_col(v):
+        return col_of(other, v)
 
     def w_rows(first):
         return pl.ds(lax.div(first, KC // 2), 2)
@@ -153,16 +163,20 @@
 
     def o_spare(n, h):
         rows = pl.ds(o_chunk(O_WIDE) * KC + h * PAIR * 2, PAIR * 2)
-        return pltpu.make_async_copy(wo_rows.at[rows, span(own_half + n * NB, NB)], bbuf.at[:, span((2 * n + h) * NB, NB)], spare_sem.at[n, h])
+        return pltpu.make_async_copy(wo_rows.at[rows, span(own_col(n * NB), NB)], bbuf.at[:, span((2 * n + h) * NB, NB)], spare_sem.at[n, h])
 
     def d_place(i):
         first = i < D_FIRST
-        n = jnp.where(first, lax.rem(i, BLOCKS_N), lax.div(i - D_FIRST, D_REST))
-        return n, jnp.where(first, lax.div(i, BLOCKS_N), D_OWN + lax.rem(i - D_FIRST, D_REST))
+        n = jnp.where(first, lax.rem(i, D_BLOCKS), lax.div(i - D_FIRST, D_REST))
+        return n, jnp.where(first, lax.div(i, D_BLOCKS), D_OWN + lax.rem(i - D_FIRST, D_REST))
 
     def d_chunk(kk):
         mine = color * D_REST + jnp.where(core == 0, kk, D_OWN - 1 - kk)
         return jnp.where(kk < D_OWN, mine, jnp.where(kk == D_OWN, D_OWN, (other_color * D_REST) + kk - D_REST))
+
+    def d_source(i, first, count):
+        n, kk = d_place(i)
+        return wd.at[w_rows(d_chunk(kk) * KC), :, :, span(color * HALF + core * QUARTER + n * NB + first, count)]
 
     other_color = 1 - color
 
@@ -178,15 +192,14 @@
         @pl.when((n >= Q_TRIPS) & (n < Q_TRIPS + O_SLOTS))
         def _():
             i = n - Q_TRIPS
-            src = wo.at[w_rows(o_chunk(lax.rem(i, O_WIDE)) * KC), :, :, span(own_half + lax.div(i, O_WIDE) * NB, NB)]
+            src = wo.at[w_rows(o_chunk(lax.rem(i, O_WIDE)) * KC), :, :, span(own_col(lax.div(i, O_WIDE) * NB), NB)]
             pltpu.make_async_copy(src, w2.at[slot], w2_sem.at[slot]).start()
 
-        @pl.when((n >= Q_TRIPS + O_SLOTS) & (n < Q_TRIPS + O_SLOTS + D_SLOTS - D_EXTRA))
+        @pl.when((n >= Q_TRIPS + O_SLOTS) & (n < Q_TRIPS + O_SLOTS + len(D_WIDE)))
         def _():
-            i = n - (Q_TRIPS + O_SLOTS)
-            block, kk = d_place(jnp.where(i < N2, i, i + D_EXTRA))
-            src = wd.at[w_rows(d_chunk(kk) * KC), :, :, span(own_half + block * NB, NB)]
-            pltpu.make_async_copy(src, w2.at[slot], w2_sem.at[slot]).start()
+            j = n - (Q_TRIPS + O_SLOTS)
+            i = jnp.where(j < D_WIDE[N2 - 2] + 1, j, jnp.where(j == N2 - 1, D_WIDE[N2 - 1], j + (D_WIDE[N2] - N2)))
+            pltpu.make_async_copy(d_source(i, 0, NB), w2.at[slot], w2_sem.at[slot]).start()
 
     def w2_wait(n):
         slot = lax.rem(n, N2)
@@ -197,7 +210,7 @@
         return w2[slot].reshape(KC, NB)
 
     def g_cols(t):
-        return pl.multiple_of(jnp.where(t < BP, own_half, sib_half) + lax.rem(t, BP) * BC, BC)
+        return pl.multiple_of(col_of(jnp.where(t < BP, core, other), lax.rem(t, BP) * BC), BC)
 
     def w1_start(n):
         slot = lax.rem(n, N1)
@@ -210,10 +223,10 @@
 
         @pl.when(n >= G_SLOTS)
         def _():
-            block, kk = d_place(n - G_SLOTS + N2)
+            u = n - G_SLOTS
+            i = jnp.where(u < SIDE, D_NARROW[0] + u, jnp.where(u < N1, D_NARROW[SIDE] - SIDE + u, D_NARROW[N1] - N1 + u))
             for h in range(2):
-                src = wd.at[w_rows(d_chunk(kk) * KC), :, :, span(own_half + block * NB + h * BC, BC)]
-                pltpu.make_async_copy(src, w1.at[slot, pl.ds(2 * h, 2), :, :, span(0, BC)], w1_sem.at[slot]).start()
+                pltpu.make_async_copy(d_source(i, h * BC, BC), w1.at[slot, pl.ds(2 * h, 2), :, :, span(0, BC)], w1_sem.at[slot]).start()
 
     def w1_wait(n):
         slot = lax.rem(n, N1)
@@ -523,7 +536,7 @@
             o_spare(n, h).wait()
         for b in range(0, NB, QL):
             out = sum(p(slice(b, b + QL)) for p in parts)
-            cols = span(own_half + n * NB + b, QL)
+            cols = span(own_col(n * NB) + b, QL)
             h = (x128[:, cols].astype(F32) + out).astype(BF16)
             x128[:, cols] = h
             hf = h.astype(F32)
@@ -550,22 +563,23 @@
     ss_copy = to_sib(ss.at[core], ss.at[core], sss_sem, ssr_sem)
     ss_copy.start()
     gacc[...] = jnp.zeros_like(gacc)
+    acc[...] = jnp.zeros_like(acc)
     ss_copy.wait()
     inv_h = lax.rsqrt(jnp.sum(ss[0] + ss[1], axis=1, keepdims=True) / MODEL + NORM_EPS)
 
-    def b_copy(i, half=own_half):
-        part = bbuf.at[pair_rows, span(half + i * BC, BC)]
+    def b_copy(i, col=own_col):
+        part = bbuf.at[pair_rows, span(col(i * BC), BC)]
         return to_sib(part, part, bs_sem.at[i], br_sem.at[i])
 
     def n_copy(cross, i, g):
         dim, k = NEIGHBOURS[g]
-        cols = span(own_half + i * BC, BC)
+        cols = span(own_col(i * BC), BC)
         return remote(bbuf.at[pl.ds(g * GROUP, GROUP), cols], bbuf.at[pl.ds(PAIR + g * GROUP, GROUP), cols],
                       ns_sem.at[cross, i, g], nr_sem.at[cross, i, g], peer(dim, k, other if cross else core))
 
     def n_arrival(cross, i, g):
         dim, k = NEIGHBOURS[g]
-        dst = bbuf.at[pl.ds(PAIR + g * GROUP, GROUP), span((sib_half if cross else own_half) + i * BC, BC)]
+        dst = bbuf.at[pl.ds(PAIR + g * GROUP, GROUP), span((sib_col if cross else own_col)(i * BC), BC)]
         return remote(dst, dst, ns_sem.at[cross, i, g], nr_sem.at[cross, i, g], peer(dim, SIDE - k, other if cross else core))
 
     pl.semaphore_wait(free_sem, 2 * len(NEIGHBOURS))
@@ -573,7 +587,7 @@
     @pl.loop(0, BP)
     def _(i):
         for j in range(BC // LANES):
-            tile = core * (HALF // LANES) + i * (BC // LANES) + j
+            tile = lax.div(own_col(i * BC), LANES) + j
             cols = span(tile * LANES)
             bbuf[pair_rows, cols] = (x128[:, cols].astype(F32) * inv_h * gains[1, pl.ds(tile, 1), :]).astype(BF16)
         for g in GROUPS:
@@ -584,6 +598,20 @@
     def _(i):
         for g in GROUPS:
             n_copy(1, i, g).start()
+
+    def h_copy(g):
+        dim, k = NEIGHBOURS[g]
+        rows = pl.ds(g * GROUP, GROUP)
+        return remote(x128.at[rows, span(other_color * HALF + core * QUARTER, QUARTER)], x128.at[rows, span(other_color * HALF + other * QUARTER, QUARTER)],
+                      hs_sem.at[g], hr_sem.at[g], peer(dim, k))
+
+    def h_arrival(g):
+        dim, k = NEIGHBOURS[g]
+        dst = x128.at[pl.ds(g * GROUP, GROUP), span(color * HALF + other * QUARTER, QUARTER)]
+        return remote(dst, dst, hs_sem.at[g], hr_sem.at[g], peer(dim, SIDE - k))
+
+    for g in GROUPS:
+        h_copy(g).start()
 
     def gate_up(rows, t, slots):
         parts = [(bbuf[rows, span(g_cols(t) + u * KC, KC)], s) for u, s in enumerate(slots)]
@@ -626,46 +654,85 @@
 
         @pl.when(t >= BP)
         def _():
-            b_copy(t - BP, sib_half).wait_recv()
+            b_copy(t - BP, sib_col).wait_recv()
             for g in GROUPS:
                 n_arrival(1, t - BP, g).wait_recv()
 
         gate_up(slice(0, 2 * PAIR), t, [w1_wait(2 * t + u) for u in range(2)])
         refill(t)
 
-    def gated(rows, j):
-        g = gacc[rows, span(j * LANES)]
-        return (g * (1.0 / (1.0 + jnp.exp(-g))) * gacc[rows, span(FFQ + j * LANES)]).astype(BF16)
-
-    @pl.loop(0, FFQ // LANES)
-    def _(j):
-        mst[:, span(j * LANES)] = gated(pl.ds(PAIR, PAIR), j)
-
-    def nm_copy(cross, g):
+    def gated(rows):
+        @pl.loop(0, FFQ // LANES)
+        def _(j):
+            g = gacc[rows, span(j * LANES)]
+            mbuf[rows, span(hidden + j * LANES)] = (g * (1.0 / (1.0 + jnp.exp(-g))) * gacc[rows, span(FFQ + j * LANES)]).astype(BF16)
+
+    def kind_rows(kind, g):
+        return pl.ds(kind * PAIR + g * GROUP, GROUP)
+
+    def m_send(kind, g):
         dim, k = NEIGHBOURS[g]
-        return remote(mst.at[pl.ds(g * GROUP, GROUP), :], mbuf.at[pl.ds(g * GROUP, GROUP), span(hidden, FFQ)],
-                      nms_sem.at[cross, g], nmr_sem.at[cross, g], peer(dim, SIDE - k, other if cross else core))
-
-    def nm_arrival(cross, g):
+        cols = span(hidden, FFQ)
+        return remote(mbuf.at[kind_rows(kind, g), cols], mbuf.at[kind_rows(1 - kind, g), cols], nms_sem.at[kind, g], nmr_sem.at[1 - kind, g],
+                      peer(dim, k if kind == 0 else SIDE - k))
+
+    def m_place(kind, g, c):
+        return mbuf.at[kind_rows(kind, g), span(other_color * FFH + c * FFQ, FFQ)]
+
+    def m_arrival(kind, g):
         dim, k = NEIGHBOURS[g]
-        dst = mbuf.at[pl.ds(g * GROUP, GROUP), span(other_color * FFH + (other if cross else core) * FFQ, FFQ)]
-        return remote(dst, dst, nms_sem.at[cross, g], nmr_sem.at[cross, g], peer(dim, k, other if cross else core))
-
-    for cross in range(2):
-        for g in GROUPS:
-            nm_copy(cross, g).start()
-
-    @pl.loop(0, FFQ // LANES)
-    def _(j):
-        mbuf[:, span(hidden + j * LANES)] = gated(pair_rows, j)
+        dst = m_place(kind, g, core)
+        return remote(dst, dst, nms_sem.at[kind, g], nmr_sem.at[kind, g], peer(dim, k if kind == 0 else SIDE - k))
+
+    def m_pass_on(kind, g, c=core):
+        part = m_place(kind, g, c)
+        return to_sib(part, part, fms_sem.at[kind, g], fmr_sem.at[kind, g])
 
     def m_copy(of_core):
         part = mbuf.at[:, span(color * FFH + of_core * FFQ, FFQ)]
         return to_sib(part, part, ms_sem, mr_sem)
 
+    for kind in (1, 0):
+        gated(pl.ds(kind * PAIR, PAIR))
+        for g in GROUPS:
+            m_send(kind, g).start()
     m_copy(core).start()
 
-    acc[...] = jnp.zeros_like(acc)
+    def d_rows(rows, kk):
+        return mbuf[rows, span(d_chunk(kk) * KC, KC)]
+
+    def first_product(kk, weights):
+        a = d_rows(slice(0, 2 * PAIR), kk)
+        for n, weight in enumerate(weights):
+            for b in range(0, NB, QL):
+                out = dot(a, weight(slice(b, b + QL)))
+                for r in range(2):
+                    acc[2 * n + r, :, b:b + QL] += out[r * PAIR:(r + 1) * PAIR]
+
+    def of_wide(slot):
+        return lambda cols: w2[slot, :, :, :, cols].reshape(KC, QL)
+
+    def of_narrow(slot):
+        return lambda cols: w1[slot, cols.start // BC * 2:cols.start // BC * 2 + 2, :, :, cols.start % BC:cols.start % BC + QL].reshape(KC, QL)
+
+    @pl.loop(0, SIDE)
+    def _(kk):
+        @pl.when(kk == 2)
+        def _():
+            m_copy(core).wait_send()
+            m_copy(other).wait_recv()
+
+        places = [Q_TRIPS + O_SLOTS + 2 * kk + u for u in range(2)]
+        first_product(kk, [of_wide(w2_wait(n)) for n in places])
+        for n in places:
+            w2_start(n + N2)
+
+    for kk in range(SIDE, D_OWN):
+        places = [G_SLOTS + 2 * (kk - SIDE) + u for u in range(2)]
+        first_product(kk, [of_narrow(w1_wait_down(n)) for n in places])
+        for n in places:
+            if n + N1 < G_SLOTS + len(D_NARROW):
+                w1_start(n + N1)
 
     @pl.loop(0, BP)
     def _(i):
@@ -674,66 +741,95 @@
             for g in GROUPS:
                 n_copy(cross, i, g).wait_send()
 
-    def z_cols(n, half=own_half):
-        return span(half + n * NB, NB)
-
-    def z_local(n):
-        return pltpu.make_async_copy(bbuf.at[own_rows, z_cols(n)], z_hbm.at[:, z_cols(n)], zl_sem.at[n])
-
-    def z_remote(n, half=own_half):
-        return to_sib(bbuf.at[sib_rows, z_cols(n)], z_hbm.at[:, z_cols(n, half)], zs_sem.at[n], zr_sem.at[n])
-
-    def down(i, weight):
-        n, kk = d_place(i)
-        a = mbuf[:, span(d_chunk(kk) * KC, KC)]
-        acc[n] += dot(a, weight)
-
-    @pl.loop(0, N2)
-    def _(i):
-        @pl.when(i == 2 * BLOCKS_N)
-        def _():
-            m_copy(core).wait_send()
-            m_copy(other).wait_recv()
-
-        down(i, wide(w2_wait(Q_TRIPS + O_SLOTS + i)))
-        w2_start(Q_TRIPS + O_SLOTS + i + N2)
-
-    @pl.loop(0, D_EXTRA)
-    def _(i):
-        slot = w1_wait_down(G_SLOTS + i)
-        down(i + N2, jnp.concatenate([w1[slot, 2 * h:2 * h + 2, :, :, :BC].reshape(KC, BC) for h in range(2)], axis=1))
-
-    @pl.loop(N2, D_SLOTS - D_EXTRA)
-    def _(j):
-        i = j + D_EXTRA
-
-        @pl.when(i == D_FIRST)
-        def _():
-            for cross in range(2):
-                for g in GROUPS:
-                    nm_arrival(cross, g).wait_recv()
-
-        down(i, wide(w2_wait(Q_TRIPS + O_SLOTS + j)))
-        w2_start(Q_TRIPS + O_SLOTS + j + N2)
-        n, kk = d_place(i)
-
-        @pl.when(kk == D_CHUNKS - 1)
-        def _():
-            @pl.loop(0, NB // QL)
-            def _(b):
-                cols = span(own_half + n * NB + b * QL, QL)
-                bbuf[pair_rows, cols] = (x128[:, cols].astype(F32) + acc[n, :, span(b * QL, QL)]).astype(BF16)
-
-            z_local(n).start()
-            z_remote(n).start()
-
-    for n in range(BLOCKS_N):
-        z_local(n).wait()
-        z_remote(n).wait_send()
-        z_remote(n, sib_half).wait_recv()
-    for cross in range(2):
+    for kind in (1, 0):
         for g in GROUPS:
-            nm_copy(cross, g).wait_send()
+            m_arrival(kind, g).wait_recv()
+            m_pass_on(kind, g).start()
+    for g in GROUPS:
+        h_copy(g).wait_send()
+        h_arrival(g).wait_recv()
+    for kind in range(2):
+        for g in GROUPS:
+            m_pass_on(kind, g).wait_send()
+            m_pass_on(kind, g, other).wait_recv()
+
+    def d_slots(n, wait):
+        found = []
+        for i in range(D_FIRST + n * D_REST, D_FIRST + (n + 1) * D_REST):
+            if i in D_WIDE:
+                place = Q_TRIPS + O_SLOTS + D_WIDE.index(i)
+                found.append((i, w2, place % N2))
+                if wait:
+                    w2_wait(place)
+            else:
+                place = G_SLOTS + D_NARROW.index(i)
+                found.append((i, w1, place % N1))
+                if wait:
+                    w1_wait_down(place)
+        return found
+
+    def d_cols(n, h, to_core=core, of_color=color):
+        return span(of_color * HALF + to_core * QUARTER + n * NB + h * BC, BC)
+
+    def second_product(kind, n, h, found):
+        for b in range(0, BC, QL):
+            out = acc[2 * n + kind, :, span(h * BC + b, QL)]
+            for i, ring, slot in found:
+                if ring is w2:
+                    weight = w2[slot, :, :, :, span(h * BC + b, QL)]
+                else:
+                    weight = w1[slot, pl.ds(2 * h, 2), :, :, b:b + QL]
+                out += dot(d_rows(pl.ds(kind * PAIR, PAIR), d_place(i)[1]), weight.reshape(KC, QL))
+            place = n * NB + h * BC + b
+            residual = x128[:, span(color * HALF + (other if kind else core) * QUARTER + place, QL)]
+            bbuf[pl.ds(kind * PAIR, PAIR), span(color * HALF + core * QUARTER + place, QL)] = (residual.astype(F32) + out).astype(BF16)
+
+    def z_away(n, h, g):
+        dim, k = NEIGHBOURS[g]
+        dst = z_hbm.at[pl.ds(g % 2 * GROUP, GROUP), d_cols(n, h)]
+        return remote(bbuf.at[kind_rows(1, g), d_cols(n, h)], dst, za_sem.at[n, h, g], zb_sem.at[core, n, h, g % 2], peer(dim, SIDE - k, g // 2))
+
+    def z_back(c, n, h, i):
+        part = z_hbm.at[pl.ds(i * GROUP, GROUP), d_cols(n, h, c, other_color)]
+        return to_sib(part, part, za_sem.at[n, h, i], zb_sem.at[c, n, h, i])
+
+    def z_local(n, h):
+        return pltpu.make_async_copy(bbuf.at[own_rows, d_cols(n, h)], z_hbm.at[:, d_cols(n, h)], zl_sem.at[n, h])
+
+    def z_remote(n, h, c=core):
+        return to_sib(bbuf.at[sib_rows, d_cols(n, h, c)], z_hbm.at[:, d_cols(n, h, c)], zs_sem.at[n, h], zr_sem.at[n, h])
+
+    for n in range(D_BLOCKS):
+        found = d_slots(n, True)
+
+        @pl.loop(0, 2)
+        def _(h):
+            second_product(1, n, h, found)
+            for g in GROUPS:
+                z_away(n, h, g).start()
+
+    for n in range(D_BLOCKS):
+        found = d_slots(n, False)
+
+        @pl.loop(0, 2)
+        def _(h):
+            second_product(0, n, h, found)
+            z_local(n, h).start()
+            z_remote(n, h).start()
+
+    for n in range(D_BLOCKS):
+        for h in range(2):
+            z_local(n, h).wait()
+            z_remote(n, h).wait_send()
+            z_remote(n, h, other).wait_recv()
+            for g in GROUPS:
+                z_away(n, h, g).wait_send()
+            for c in range(2):
+                for i in range(2):
+                    z_back(c, n, h, i).wait_recv()
+    for kind in range(2):
+        for g in GROUPS:
+            m_send(kind, g).wait_send()
     for s in stores:
         s.wait()
 
@@ -773,7 +869,8 @@
             'gs': (len(BLOCKS), len(SENDS), len(STEPS_ALONG)), 'gr': (len(BLOCKS), len(SENDS), len(STEPS_ALONG)),
             'fs': (len(BLOCKS), len(SENDS) + 1, len(STEPS_ALONG)), 'fr': (len(BLOCKS), len(SENDS) + 1, len(STEPS_ALONG)),
             'os': (), 'or': (), 'sss': (), 'ssr': (), 'bs': (BP,), 'br': (BP,), 'ns': (2, BP, len(GROUPS)), 'nr': (2, BP, len(GROUPS)),
-            'ms': (), 'mr': (), 'nms': (2, len(GROUPS)), 'nmr': (2, len(GROUPS)), 'zl': (BLOCKS_N,), 'zs': (BLOCKS_N,), 'zr': (BLOCKS_N,), 'ko': (2,), 'spare': (BLOCKS_N, 2),
+            'ms': (), 'mr': (), 'nms': (2, len(GROUPS)), 'nmr': (2, len(GROUPS)), 'fms': (2, len(GROUPS)), 'fmr': (2, len(GROUPS)), 'hs': (len(GROUPS),), 'hr': (len(GROUPS),),
+            'za': (D_BLOCKS, 2, len(GROUPS)), 'zb': (2, D_BLOCKS, 2, 2), 'zl': (D_BLOCKS, 2), 'zs': (D_BLOCKS, 2), 'zr': (D_BLOCKS, 2), 'ko': (2,), 'spare': (BLOCKS_N, 2),
         }
 
         def dma(shape):
@@ -793,8 +890,7 @@
                 pltpu.VMEM((2, HEAD_DIM, QL), BF16),
                 *(pltpu.VMEM(s, F32) for s in stats),
                 pltpu.VMEM((2, PAIR, QCOLS), BF16),
-                pltpu.VMEM((PAIR, FF), BF16),
-                pltpu.VMEM((PAIR, FFQ), BF16),
+                pltpu.VMEM((2 * PAIR, FF), BF16),
                 pltpu.VMEM((2, ROWS, LANES), F32),
                 pltpu.VMEM((2, PAIR, LANES), F32),
                 pltpu.VMEM((2, ROWS, LANES), BF16),

time: 118 us -> 110 us (0.932)
  Pallas kernels: 118 us -> 109 us
    pallas_call x1, Pallas kernels: 115 us -> 107 us  [device_fn(): pl.pallas_call(layer_kernel, out_shape=outs, in_specs=[any_space, vmem, v...]
where the time goes in v3:
time: 110 us
  Pallas kernels  109 us (99%)
    pallas_call x1, Pallas kernels, device_fn(): pl.pallas_call(layer_kernel, out_shape=outs, in_specs=[any_space, vmem, v...  107 us
    pallas_call x1, Pallas kernels, device_fn(): pl.pallas_call(deliver_kernel, out_shape=outs, in_specs=[any_space] * len...  2.49 us

profile of v3, /device:TPU:1, one launch (start us, length us, event | category | flops | bytes accessed | tf_op | source)
XLA Modules:
  0.0 110.1 jit_solution(11948023627152055363)
XLA Ops:
  0.6 106.8 %layer.1 = (bf16[64,16384]{1,0:T(8,128)(2,1)}, bf16[64,128]{1,0:T(8,128)(2,1)}, bf16[64,128]{1,0:T(8,128)(2,1)}) custom-call(bf16[64,16384]{1,0:T(8,128)(2,1)} %bitcast.16, s32[1,64]{1,0:T(1,128)} %bitcast.19, bf16[128,128]{1,0:T(8,128)(2,1)} %bitcast.17, bf16[64,4,64,2048]{3,2,1,0:T(8,128)(2,1)} %bitcast.3.wq, bf16[64,4,64,128]{3,2,1,0:T(8,128)(2,1)} %bitcast.14, ...), custom_call_target="tpu_custom_call" | custom-call | tf_op jit(solution)/shard_map/layer/pallas_call | solution.py:879
  107.4 2.5 %finish.1 = (bf16[64,16384]{1,0:T(8,128)(2,1)}, bf16[64,128]{1,0:T(8,128)(2,1)}, bf16[64,128]{1,0:T(8,128)(2,1)}) custom-call(bf16[64,16384]{1,0:T(8,128)(2,1)} %get-tuple-element.9.z_in, bf16[64,128]{1,0:T(8,128)(2,1)} %get-tuple-element.10.k_in, bf16[64,128]{1,0:T(8,128)(2,1)} %get-tuple-element.11.v_in), custom_call_target="tpu_custom_call" | custom-call | tf_op jit(solution)/shard_map/finish/pallas_call | solution.py:906

commit v4 on v3

--- a/solution.py
+++ b/solution.py
@@ -50,23 +50,29 @@
 D_BLOCKS = QUARTER // NB
 D_FIRST = D_OWN * D_BLOCKS
 D_SLOTS = D_CHUNKS * D_BLOCKS
-D_WIDE = tuple(range(8)) + (12,) + tuple(range(15, 23))
-D_NARROW = tuple(range(8, 12)) + (13, 14, 23, 24, 25)
+D_NARROW = (8, 9, 10, 11, 13, 14, 23, 24, 25)
 G_SLOTS = MODEL // KC
 G_TRIPS = G_SLOTS // 2
+G_NARROW = G_SLOTS - 2
 BC = 2 * KC
 BP = HALF // BC
 XP = 4
 PIECES_PER_SLOT = FFQ // LANES
 KV_PIECES = MODEL // KC
 KV_UNROLL = 8
-HOOK_B, HOOK_C = 0, 12
-PRE = 2
+HOOK_B, HOOK_C = 0, 11
+PRE = 3
+WIDE_D = Q_TRIPS + O_SLOTS
+D_EARLY = 5
+WIDE_G = WIDE_D + D_EARLY
+WIDE_LATE = WIDE_G + N2
+D_LATE = 3
+D_KEPT = 12
 QL = 512
 SCORE_BUFS = (0, 2 * QL)
 NEAR = 6
 STEPS = 18
-DELIVER = 4096
+DELIVER = 2048
 NEIGHBOURS = (('x', 1), ('x', 3), ('y', 1), ('y', 3))
 GROUPS = range(len(NEIGHBOURS))
 GROUP = PAIR // len(NEIGHBOURS)
@@ -79,6 +85,7 @@
 SENDS = ((OWN, 0), (OWN, 1), (OWN, 2), ((1, 0, 0), 1), ((1, 0, 0), 2), ((0, 1, 0), 2), ((1, 1, 0), 2))
 ROUNDS = ((0, 1, 2), (3, 4, 5), (6,))
 STEPS_ALONG = (1, 2, 3)
+BOTH = range(2)
 
 
 def dot(a, b):
@@ -185,7 +192,7 @@
 
         @pl.when(n < Q_TRIPS)
         def _():
-            for h in range(2):
+            for h in BOTH:
                 src = wq.at[w_rows(n * (2 * KC) + h * KC), :, :, span(core * QCOLS, QCOLS)]
                 pltpu.make_async_copy(src, w2.at[slot, :, :, :, pl.ds(h * QCOLS, QCOLS)], w2_sem.at[slot]).start()
 
@@ -195,11 +202,26 @@
             src = wo.at[w_rows(o_chunk(lax.rem(i, O_WIDE)) * KC), :, :, span(own_col(lax.div(i, O_WIDE) * NB), NB)]
             pltpu.make_async_copy(src, w2.at[slot], w2_sem.at[slot]).start()
 
-        @pl.when((n >= Q_TRIPS + O_SLOTS) & (n < Q_TRIPS + O_SLOTS + len(D_WIDE)))
-        def _():
-            j = n - (Q_TRIPS + O_SLOTS)
-            i = jnp.where(j < D_WIDE[N2 - 2] + 1, j, jnp.where(j == N2 - 1, D_WIDE[N2 - 1], j + (D_WIDE[N2] - N2)))
+        @pl.when((n >= WIDE_G) & (n < WIDE_D + N2))
+        def _():
+            u = n - WIDE_G
+            rows = w_rows(g_cols(PRE) + lax.div(u, 2) * KC)
+            for i, w in enumerate((wg, wu)):
+                @pl.when(lax.rem(u, 2) == i)
+                def _():
+                    pltpu.make_async_copy(w.at[rows, :, :, span(hidden, FFQ)], w2.at[slot, :, :, :, pl.ds(0, FFQ)], w2_sem.at[slot]).start()
+
+        @pl.when((n >= WIDE_D) & ((n < WIDE_G) | (n >= WIDE_D + N2)))
+        def _():
+            late = n - (WIDE_D + N2) + D_KEPT + D_LATE
+            i = jnp.where(n < WIDE_G, n - WIDE_D, jnp.where(n < WIDE_LATE, late, jnp.where(n < WIDE_LATE + D_LATE, n - WIDE_LATE + D_EARLY, jnp.where(
+                n == WIDE_LATE + D_LATE, D_KEPT, n - (WIDE_LATE + N2) + D_KEPT + D_LATE + D_EARLY))))
             pltpu.make_async_copy(d_source(i, 0, NB), w2.at[slot], w2_sem.at[slot]).start()
+
+    def d_wide(i):
+        if isinstance(i, int) and i >= D_KEPT:
+            return WIDE_LATE + D_LATE if i == D_KEPT else i - D_KEPT - D_LATE + (WIDE_D + N2 if i < D_KEPT + D_LATE + D_EARLY else WIDE_LATE + N2 - D_EARLY)
+        return jnp.where(i < D_EARLY, WIDE_D + i, WIDE_LATE - D_EARLY + i)
 
     def w2_wait(n):
         slot = lax.rem(n, N2)
@@ -215,17 +237,19 @@
     def w1_start(n):
         slot = lax.rem(n, N1)
 
-        @pl.when(n < G_SLOTS)
-        def _():
+        @pl.when(n < G_NARROW)
+        def _():
+            t = lax.div(n, 2)
+            first = g_cols(jnp.where(t < PRE, t, t + 1))
             for i, w in enumerate((wg, wu)):
-                src = w.at[w_rows(g_cols(lax.div(n, 2)) + lax.rem(n, 2) * KC), :, :, span(hidden, FFQ)]
+                src = w.at[w_rows(first + lax.rem(n, 2) * KC), :, :, span(hidden, FFQ)]
                 pltpu.make_async_copy(src, w1.at[slot, pl.ds(2 * i, 2)], w1_sem.at[slot]).start()
 
-        @pl.when(n >= G_SLOTS)
-        def _():
-            u = n - G_SLOTS
+        @pl.when(n >= G_NARROW)
+        def _():
+            u = n - G_NARROW
             i = jnp.where(u < SIDE, D_NARROW[0] + u, jnp.where(u < N1, D_NARROW[SIDE] - SIDE + u, D_NARROW[N1] - N1 + u))
-            for h in range(2):
+            for h in BOTH:
                 pltpu.make_async_copy(d_source(i, h * BC, BC), w1.at[slot, pl.ds(2 * h, 2), :, :, span(0, BC)], w1_sem.at[slot]).start()
 
     def w1_wait(n):
@@ -247,7 +271,7 @@
 
     @pl.loop(0, KV_PIECES)
     def _(c):
-        for i in range(2):
+        for i in BOTH:
             kv_copy(c, i).start()
 
     def x_copy(i):
@@ -287,21 +311,21 @@
 
     normalize(own_rows, inv_own, 0, MODEL // BC)
 
+    def kv_trip(i, total):
+        places = [i * KV_UNROLL + u for u in range(KV_UNROLL)]
+        for c in places:
+            for j in BOTH:
+                kv_copy(c, j).wait()
+        for c in places:
+            w = jnp.concatenate([kv_dst(c, j)[...].reshape(KC, LANES) for j in BOTH], axis=1)
+            total = total + dot(bbuf[own_rows, span(c * KC, KC)], w)
+        return total
+
+    kv_raw = lax.fori_loop(0, KV_PIECES // KV_UNROLL, kv_trip, jnp.zeros((ROWS, 2 * LANES), F32))
     @pl.loop(0, N2)
     def _(n):
         w2_start(n)
 
-    def kv_trip(i, total):
-        places = [i * KV_UNROLL + u for u in range(KV_UNROLL)]
-        for c in places:
-            for j in range(2):
-                kv_copy(c, j).wait()
-        for c in places:
-            w = jnp.concatenate([kv_dst(c, j)[...].reshape(KC, LANES) for j in range(2)], axis=1)
-            total = total + dot(bbuf[own_rows, span(c * KC, KC)], w)
-        return total
-
-    kv_raw = lax.fori_loop(0, KV_PIECES // KV_UNROLL, kv_trip, jnp.zeros((ROWS, 2 * LANES), F32))
     r0 = (pl.multiple_of(core * CHUNK, CHUNK), pl.multiple_of(other * CHUNK, CHUNK))
     stores = []
     for i, (t, out) in enumerate(((rope(kv_raw[:, :LANES], cos_own, sin_own), k_out), (kv_raw[:, LANES:], v_out))):
@@ -411,14 +435,14 @@
         w2_start(i + N2)
 
     for n in range(BLOCKS_N):
-        for h in range(2):
+        for h in BOTH:
             o_spare(n, h).start()
 
     @pl.loop(0, K_SLOT)
     def _(n):
         w1_start(n)
 
-    pos_all = jnp.concatenate([st[i][:, 1:2] for i in range(2)], axis=0)
+    pos_all = jnp.concatenate([st[i][:, 1:2] for i in BOTH], axis=0)
     cos_t, sin_t = rope_tables(pos_all)
     EARLY = (slice(0, CHUNK), slice(ROWS, ROWS + CHUNK))
     LATE = (slice(ROWS + CHUNK, PAIR), slice(CHUNK, ROWS))
@@ -460,7 +484,7 @@
         plane = lax.rem(cz + dz, SIDE) * SIDE
         u = iota(ROWS, 1, 0)
         tops = [jnp.full((SUBLANES, LANES), NEG_BIG, F32)] * SIDE
-        for part in range(2):
+        for part in BOTH:
             keys = w1[K_SLOT, dy + part, :, :, lanes].reshape(SIDE * ROWS, LANES)
             row_y = (plane + lax.rem(cy + dy + part, SIDE)) * SIDE
             scores = dot(keys, q)
@@ -481,7 +505,7 @@
         m_old = ml[qh, 0, :1]
         m_new = jnp.maximum(m_old, jnp.max(mx[buf], axis=0, keepdims=True))
         shift = m_new * EXP_SCALE
-        p = jnp.concatenate([jnp.exp2(gacc[:, span(SCORE_BUFS[buf] + i * QL, QL)] * EXP_SCALE - shift) for i in range(2)], axis=0)
+        p = jnp.concatenate([jnp.exp2(gacc[:, span(SCORE_BUFS[buf] + i * QL, QL)] * EXP_SCALE - shift) for i in BOTH], axis=0)
         alpha = jnp.exp2((m_old - m_new) * EXP_SCALE)
         ml[qh, 0, :1] = m_new
         ml[qh, 1, :1] = ml[qh, 1, :1] * alpha + jnp.sum(p, axis=0, keepdims=True)
@@ -506,7 +530,7 @@
     for hp in range(PAIR_HEADS):
         for half, rows in enumerate((EARLY, LATE)):
             o = (acc[half, :, span(hp * LANES)] / ml[half, 1, :1, span(hp * LANES)]).T.astype(BF16)
-            for u in range(2):
+            for u in BOTH:
                 for i, r in enumerate(rows):
                     obuf[core, r, span((2 * hp + u) * LANES)] = o[ROWS * u + CHUNK * i:ROWS * u + CHUNK * (i + 1)]
     o_copy = to_sib(obuf.at[core], obuf.at[core], os_sem, or_sem)
@@ -517,13 +541,13 @@
 
     def o_part(n, own):
         group = core if own else other
-        places = range(2) if own else range(2, O_WIDE)
+        places = BOTH if own else range(2, O_WIDE)
         slots = [w2_wait(Q_TRIPS + O_WIDE * n + u) for u in places]
 
         def part(cols):
             terms = [dot(obuf[group, :, u % 2 * KC:(u % 2 + 1) * KC], w2[s, :, :, :, cols].reshape(KC, QL)) for u, s in zip(places, slots)]
             if not own:
-                for h in range(2):
+                for h in BOTH:
                     w = bbuf[:, span((2 * n + h) * NB + cols.start, QL)]
                     terms.append(dot(obuf[group, :, span(KC + h * PAIR * 2, PAIR * 2)], w))
             return sum(terms)
@@ -532,7 +556,7 @@
 
     def o_block(n, parts):
         total = jnp.zeros((PAIR, LANES), F32)
-        for h in range(2):
+        for h in BOTH:
             o_spare(n, h).wait()
         for b in range(0, NB, QL):
             out = sum(p(slice(b, b + QL)) for p in parts)
@@ -558,7 +582,7 @@
         o_block(n, [o_part(n, True), o_part(n, False)])
 
     for dim, k in NEIGHBOURS:
-        for c in range(2):
+        for c in BOTH:
             pl.semaphore_signal(free_sem, device_id={'cp': peer(dim, SIDE - k, c)}, device_id_type=MESH)
     ss_copy = to_sib(ss.at[core], ss.at[core], sss_sem, ssr_sem)
     ss_copy.start()
@@ -613,16 +637,19 @@
     for g in GROUPS:
         h_copy(g).start()
 
-    def gate_up(rows, t, slots):
-        parts = [(bbuf[rows, span(g_cols(t) + u * KC, KC)], s) for u, s in enumerate(slots)]
+    def narrow_part(s):
+        return lambda i, cols: w1[s, 2 * i:2 * i + 2, :, :, cols]
+
+    def gate_up(rows, t, weights):
+        parts = [(bbuf[rows, span(g_cols(t) + u * KC, KC)], w) for u, w in enumerate(weights)]
 
         def block(i, cols):
-            return [w1[s, 2 * i:2 * i + 2, :, :, cols].reshape(KC, cols.stop - cols.start) for _, s in parts]
+            return [w(i, cols).reshape(KC, cols.stop - cols.start) for _, w in parts]
 
         def product_of(weights):
             return sum(dot(a, w) for (a, _), w in zip(parts, weights))
 
-        for i in range(2):
+        for i in BOTH:
             for b in range(0, FFQ - LANES, QL):
                 gacc[rows, i * FFQ + b:i * FFQ + b + QL] += product_of(block(i, slice(b, b + QL)))
         last = slice(FFQ - LANES, FFQ)
@@ -631,21 +658,32 @@
         gacc[rows, 2 * FFQ - LANES:] += pair[:, LANES:]
 
     def refill(t):
-        for u in range(2):
+        for u in BOTH:
             w1_start(2 * t + u + N1)
 
     @pl.loop(0, PRE)
     def _(t):
-        gate_up(slice(0, PAIR), t, [w1_wait(2 * t + u) for u in range(2)])
+        gate_up(slice(0, PAIR), t, [narrow_part(w1_wait(2 * t + u)) for u in BOTH])
 
     @pl.loop(0, PRE)
     def _(t):
         for g in GROUPS:
             n_arrival(0, t, g).wait_recv()
-        gate_up(slice(PAIR, 2 * PAIR), t, [2 * t + u for u in range(2)])
+        gate_up(slice(PAIR, 2 * PAIR), t, [narrow_part(2 * t + u) for u in BOTH])
         refill(t)
 
-    @pl.loop(PRE, G_TRIPS)
+    def wide_part(n):
+        slots = [(n + i) % N2 for i in BOTH]
+        for slot in slots:
+            dst = w2.at[slot, :, :, :, pl.ds(0, FFQ)]
+            pltpu.make_async_copy(wg.at[w_rows(0), :, :, span(0, FFQ)], dst, w2_sem.at[slot]).wait()
+        return lambda i, cols: w2[slots[i], :, :, :, cols]
+
+    for g in GROUPS:
+        n_arrival(0, PRE, g).wait_recv()
+    gate_up(slice(0, 2 * PAIR), PRE, [wide_part(WIDE_G + 2 * u) for u in BOTH])
+
+    @pl.loop(PRE + 1, G_TRIPS)
     def _(t):
         @pl.when(t < BP)
         def _():
@@ -658,8 +696,13 @@
             for g in GROUPS:
                 n_arrival(1, t - BP, g).wait_recv()
 
-        gate_up(slice(0, 2 * PAIR), t, [w1_wait(2 * t + u) for u in range(2)])
-        refill(t)
+        gate_up(slice(0, 2 * PAIR), t, [narrow_part(w1_wait(2 * t - 2 + u)) for u in BOTH])
+        refill(t - 1)
+
+        @pl.when(t == G_TRIPS - 2)
+        def _():
+            for n in range(WIDE_LATE, WIDE_LATE + D_LATE + 1):
+                w2_start(n)
 
     def gated(rows):
         @pl.loop(0, FFQ // LANES)
@@ -670,32 +713,33 @@
     def kind_rows(kind, g):
         return pl.ds(kind * PAIR + g * GROUP, GROUP)
 
-    def m_send(kind, g):
+    def m_send(kind, cross, g):
         dim, k = NEIGHBOURS[g]
         cols = span(hidden, FFQ)
-        return remote(mbuf.at[kind_rows(kind, g), cols], mbuf.at[kind_rows(1 - kind, g), cols], nms_sem.at[kind, g], nmr_sem.at[1 - kind, g],
-                      peer(dim, k if kind == 0 else SIDE - k))
+        return remote(mbuf.at[kind_rows(kind, g), cols], mbuf.at[kind_rows(1 - kind, g), cols], nms_sem.at[kind, cross, g],
+                      nmr_sem.at[1 - kind, cross, g], peer(dim, k if kind == 0 else SIDE - k, other if cross else core))
 
     def m_place(kind, g, c):
         return mbuf.at[kind_rows(kind, g), span(other_color * FFH + c * FFQ, FFQ)]
 
-    def m_arrival(kind, g):
+    def m_arrival(kind, cross, g):
         dim, k = NEIGHBOURS[g]
-        dst = m_place(kind, g, core)
-        return remote(dst, dst, nms_sem.at[kind, g], nmr_sem.at[kind, g], peer(dim, k if kind == 0 else SIDE - k))
-
-    def m_pass_on(kind, g, c=core):
-        part = m_place(kind, g, c)
-        return to_sib(part, part, fms_sem.at[kind, g], fmr_sem.at[kind, g])
+        dst = m_place(kind, g, other if cross else core)
+        return remote(dst, dst, nms_sem.at[kind, cross, g], nmr_sem.at[kind, cross, g], peer(dim, k if kind == 0 else SIDE - k))
+
+    def m_pass_on(g, c=core):
+        part = m_place(0, g, c)
+        return to_sib(part, part, fms_sem.at[g], fmr_sem.at[g])
 
     def m_copy(of_core):
         part = mbuf.at[:, span(color * FFH + of_core * FFQ, FFQ)]
         return to_sib(part, part, ms_sem, mr_sem)
 
-    for kind in (1, 0):
+    for kind in BOTH:
         gated(pl.ds(kind * PAIR, PAIR))
-        for g in GROUPS:
-            m_send(kind, g).start()
+        for cross in range(2 - kind):
+            for g in GROUPS:
+                m_send(kind, cross, g).start()
     m_copy(core).start()
 
     def d_rows(rows, kk):
@@ -706,7 +750,7 @@
         for n, weight in enumerate(weights):
             for b in range(0, NB, QL):
                 out = dot(a, weight(slice(b, b + QL)))
-                for r in range(2):
+                for r in BOTH:
                     acc[2 * n + r, :, b:b + QL] += out[r * PAIR:(r + 1) * PAIR]
 
     def of_wide(slot):
@@ -722,47 +766,42 @@
             m_copy(core).wait_send()
             m_copy(other).wait_recv()
 
-        places = [Q_TRIPS + O_SLOTS + 2 * kk + u for u in range(2)]
+        places = [d_wide(2 * kk + u) for u in BOTH]
         first_product(kk, [of_wide(w2_wait(n)) for n in places])
         for n in places:
             w2_start(n + N2)
 
     for kk in range(SIDE, D_OWN):
-        places = [G_SLOTS + 2 * (kk - SIDE) + u for u in range(2)]
+        places = [G_NARROW + 2 * (kk - SIDE) + u for u in BOTH]
         first_product(kk, [of_narrow(w1_wait_down(n)) for n in places])
         for n in places:
-            if n + N1 < G_SLOTS + len(D_NARROW):
+            if n + N1 < G_NARROW + len(D_NARROW):
                 w1_start(n + N1)
 
     @pl.loop(0, BP)
     def _(i):
         b_copy(i).wait_send()
-        for cross in range(2):
+        for cross in BOTH:
             for g in GROUPS:
                 n_copy(cross, i, g).wait_send()
 
-    for kind in (1, 0):
+    for cross in BOTH:
         for g in GROUPS:
-            m_arrival(kind, g).wait_recv()
-            m_pass_on(kind, g).start()
+            m_arrival(1, cross, g).wait_recv()
     for g in GROUPS:
         h_copy(g).wait_send()
         h_arrival(g).wait_recv()
-    for kind in range(2):
-        for g in GROUPS:
-            m_pass_on(kind, g).wait_send()
-            m_pass_on(kind, g, other).wait_recv()
 
     def d_slots(n, wait):
         found = []
         for i in range(D_FIRST + n * D_REST, D_FIRST + (n + 1) * D_REST):
-            if i in D_WIDE:
-                place = Q_TRIPS + O_SLOTS + D_WIDE.index(i)
+            if i not in D_NARROW:
+                place = d_wide(i)
                 found.append((i, w2, place % N2))
                 if wait:
                     w2_wait(place)
             else:
-                place = G_SLOTS + D_NARROW.index(i)
+                place = G_NARROW + D_NARROW.index(i)
                 found.append((i, w1, place % N1))
                 if wait:
                     w1_wait_down(place)
@@ -808,6 +847,15 @@
             for g in GROUPS:
                 z_away(n, h, g).start()
 
+        if n == 0:
+            for g in GROUPS:
+                m_arrival(0, 0, g).wait_recv()
+                m_pass_on(g).start()
+
+    for g in GROUPS:
+        m_pass_on(g).wait_send()
+        m_pass_on(g, other).wait_recv()
+
     for n in range(D_BLOCKS):
         found = d_slots(n, False)
 
@@ -818,18 +866,19 @@
             z_remote(n, h).start()
 
     for n in range(D_BLOCKS):
-        for h in range(2):
+        for h in BOTH:
             z_local(n, h).wait()
             z_remote(n, h).wait_send()
             z_remote(n, h, other).wait_recv()
             for g in GROUPS:
                 z_away(n, h, g).wait_send()
-            for c in range(2):
-                for i in range(2):
+            for c in BOTH:
+                for i in BOTH:
                     z_back(c, n, h, i).wait_recv()
-    for kind in range(2):
-        for g in GROUPS:
-            m_send(kind, g).wait_send()
+    for kind in BOTH:
+        for cross in range(2 - kind):
+            for g in GROUPS:
+                m_send(kind, cross, g).wait_send()
     for s in stores:
         s.wait()
 
@@ -869,7 +918,7 @@
             'gs': (len(BLOCKS), len(SENDS), len(STEPS_ALONG)), 'gr': (len(BLOCKS), len(SENDS), len(STEPS_ALONG)),
             'fs': (len(BLOCKS), len(SENDS) + 1, len(STEPS_ALONG)), 'fr': (len(BLOCKS), len(SENDS) + 1, len(STEPS_ALONG)),
             'os': (), 'or': (), 'sss': (), 'ssr': (), 'bs': (BP,), 'br': (BP,), 'ns': (2, BP, len(GROUPS)), 'nr': (2, BP, len(GROUPS)),
-            'ms': (), 'mr': (), 'nms': (2, len(GROUPS)), 'nmr': (2, len(GROUPS)), 'fms': (2, len(GROUPS)), 'fmr': (2, len(GROUPS)), 'hs': (len(GROUPS),), 'hr': (len(GROUPS),),
+            'ms': (), 'mr': (), 'nms': (2, 2, len(GROUPS)), 'nmr': (2, 2, len(GROUPS)), 'fms': (len(GROUPS),), 'fmr': (len(GROUPS),), 'hs': (len(GROUPS),), 'hr': (len(GROUPS),),
             'za': (D_BLOCKS, 2, len(GROUPS)), 'zb': (2, D_BLOCKS, 2, 2), 'zl': (D_BLOCKS, 2), 'zs': (D_BLOCKS, 2), 'zr': (D_BLOCKS, 2), 'ko': (2,), 'spare': (BLOCKS_N, 2),
         }
 

time: 110 us -> 108 us (0.982)
  Pallas kernels: 109 us -> 107 us
    pallas_call x1, Pallas kernels: 107 us -> 105 us  [device_fn(): pl.pallas_call(layer_kernel, out_shape=outs, in_specs=[any_space, vmem, v...]
where the time goes in v4:
time: 108 us
  Pallas kernels  107 us (99%)
    pallas_call x1, Pallas kernels, device_fn(): pl.pallas_call(layer_kernel, out_shape=outs, in_specs=[any_space, vmem, v...  105 us
    pallas_call x1, Pallas kernels, device_fn(): pl.pallas_call(deliver_kernel, out_shape=outs, in_specs=[any_space] * len...  2.46 us

profile of v4, /device:TPU:1, one launch (start us, length us, event | category | flops | bytes accessed | tf_op | source)
XLA Modules:
  0.0 107.8 jit_solution(11475407228762292593)
XLA Ops:
  0.6 104.5 %layer.1 = (bf16[64,16384]{1,0:T(8,128)(2,1)}, bf16[64,128]{1,0:T(8,128)(2,1)}, bf16[64,128]{1,0:T(8,128)(2,1)}) custom-call(bf16[64,16384]{1,0:T(8,128)(2,1)} %bitcast.16, s32[1,64]{1,0:T(1,128)} %bitcast.19, bf16[128,128]{1,0:T(8,128)(2,1)} %bitcast.17, bf16[64,4,64,2048]{3,2,1,0:T(8,128)(2,1)} %bitcast.3.wq, bf16[64,4,64,128]{3,2,1,0:T(8,128)(2,1)} %bitcast.14, ...), custom_call_target="tpu_custom_call" | custom-call | tf_op jit(solution)/shard_map/layer/pallas_call | solution.py:928
  105.2 2.5 %finish.1 = (bf16[64,16384]{1,0:T(8,128)(2,1)}, bf16[64,128]{1,0:T(8,128)(2,1)}, bf16[64,128]{1,0:T(8,128)(2,1)}) custom-call(bf16[64,16384]{1,0:T(8,128)(2,1)} %get-tuple-element.9.z_in, bf16[64,128]{1,0:T(8,128)(2,1)} %get-tuple-element.10.k_in, bf16[64,128]{1,0:T(8,128)(2,1)} %get-tuple-element.11.v_in), custom_call_target="tpu_custom_call" | custom-call | tf_op jit(solution)/shard_map/finish/pallas_call | solution.py:955
